TPU v7x, 32 devices: a 4x4x1 block of a 4x4x8 slice. The times are simulated.
32 devices in a mesh: member: 1 (over z), lat: 32 (over y, x, core).
Axes of the slice: x: 4, y: 4, z: 1, core: 2. Of those that a mesh axis runs over, the one named last changes fastest.
The devices are a block of a 4x4x8 slice.
Arguments:
- field_in: float32 [8, 128, 96, 192], P('member', None, 'lat')
- grad_out: float32 [8, 128, 96, 192], P('member', None, 'lat')
- p_fwd: float32 [96, 96, 96], replicated
- p_inv: float32 [96, 96, 96], replicated
- w_mix: float32 [96, 128, 128, 2], replicated
Outputs:
- output 1: float32 [8, 128, 96, 192], P('member', None, 'lat')
- output 2: float32 [96, 128, 128, 2], P('member')
All inputs are finite; a program needn't handle non-finite values.
Results may differ from a plain program's by a relative error of at most 0.00628536.
Values are sent between devices in bfloat16 or wider.
A program may use at most 768 MiB of HBM per device.

v0:
```python
import math
import jax
import jax.numpy as jnp
from jax import lax
from jax.sharding import PartitionSpec as P


def gelu_grad(values):
    cumulative = 0.5 * (1.0 + lax.erf(values * math.sqrt(0.5)))
    density = jnp.exp(-0.5 * values * values) / math.sqrt(2.0 * math.pi)
    return cumulative + values * density


def mix_matrix(w_mix):
    w_real = w_mix[..., 0]
    w_imag = w_mix[..., 1]
    upper_half = jnp.stack([w_real, -w_imag], axis=-1)
    lower_half = jnp.stack([w_imag, w_real], axis=-1)
    return jnp.stack([upper_half, lower_half], axis=2).astype(jnp.bfloat16)


def analysis(values, mode_count, mode_gains):
    spectrum = jnp.fft.rfft(values, axis=-1)[..., :mode_count] * mode_gains
    return jnp.stack([spectrum.real, spectrum.imag], axis=-2).astype(jnp.bfloat16)


def synthesis(spec_pair, lon_count, mode_gains):
    complex_spec = lax.complex(spec_pair[..., 0, :].astype(jnp.float32), spec_pair[..., 1, :].astype(jnp.float32)) * mode_gains
    pad_width = [(0, 0)] * (complex_spec.ndim - 1) + [(0, lon_count // 2 + 1 - complex_spec.shape[-1])]
    return jnp.fft.irfft(jnp.pad(complex_spec, pad_width), n=lon_count, axis=-1)


def solution(mesh):
    lat_size = mesh.shape['lat']
    field_spec = P('member', None, 'lat', None)

    def local_step(field_loc, grad_loc, p_fwd, p_inv, w_mix):
        lon_count = field_loc.shape[-1]
        lat_count = p_fwd.shape[-1]
        m_local = lat_count // lat_size
        m_start = lax.axis_index('lat') * m_local
        root_lon = math.sqrt(lon_count)
        is_mean = jnp.arange(lat_count) == 0
        pw_own = lax.dynamic_slice_in_dim(p_fwd, m_start, m_local, axis=0).astype(jnp.bfloat16)
        pi_own = lax.dynamic_slice_in_dim(p_inv, m_start, m_local, axis=0).astype(jnp.bfloat16)
        w_big = mix_matrix(w_mix)
        four_lat = analysis(field_loc, lat_count, 1.0 / root_lon)
        four_own = lax.all_to_all(four_lat, 'lat', 4, 2, tiled=True)
        coeffs = jnp.einsum('mlt,bctrm->bclrm', pw_own, four_own, preferred_element_type=jnp.float32).astype(jnp.bfloat16)
        mixed_coef = jnp.einsum('losir,bilrm->bolsm', w_big, coeffs, preferred_element_type=jnp.float32).astype(jnp.bfloat16)
        back_own = jnp.einsum('mlt,bclrm->bctrm', pi_own, mixed_coef, preferred_element_type=jnp.float32).astype(jnp.bfloat16)
        back_lat = lax.all_to_all(back_own, 'lat', 2, 4, tiled=True)
        hidden = synthesis(back_lat, lon_count, root_lon)
        grad_hidden = grad_loc * gelu_grad(hidden)
        grad_back_lat = analysis(grad_hidden, lat_count, jnp.where(is_mean, 1.0, 2.0) / root_lon)
        grad_back_own = lax.all_to_all(grad_back_lat, 'lat', 4, 2, tiled=True)
        grad_mixed = jnp.einsum('mlt,bctrm->bclrm', pi_own, grad_back_own, preferred_element_type=jnp.float32).astype(jnp.bfloat16)
        gw_part = jnp.einsum('bolsm,bilrm->losir', grad_mixed, coeffs, preferred_element_type=jnp.float32)
        gw_total = lax.psum(gw_part, 'lat')
        grad_coef = jnp.einsum('losir,bolsm->bilrm', w_big, grad_mixed, preferred_element_type=jnp.float32).astype(jnp.bfloat16)
        grad_four_own = jnp.einsum('mlt,bclrm->bctrm', pw_own, grad_coef, preferred_element_type=jnp.float32).astype(jnp.bfloat16)
        grad_four_lat = lax.all_to_all(grad_four_own, 'lat', 2, 4, tiled=True)
        grad_field = grad_loc + synthesis(grad_four_lat, lon_count, jnp.where(is_mean, 1.0, 0.5) * root_lon)
        grad_wmix = jnp.stack([gw_total[:, :, 0, :, 0] + gw_total[:, :, 1, :, 1], gw_total[:, :, 1, :, 0] - gw_total[:, :, 0, :, 1]], axis=-1)
        return grad_field, grad_wmix

    return jax.shard_map(local_step, mesh=mesh, in_specs=(field_spec, field_spec, P(), P(), P()), out_specs=(field_spec, P('member', None, None, None)), check_vma=False)
```

profile of v0, /device:TPU:97, one launch (start us, length us, event | category | flops | bytes accessed | tf_op | source)
XLA Modules:
  0.0 483.0 jit_solution(5354978314418705178)
XLA Ops:
  16.0 6.7 %fusion.30 = f32[8,128,3,64,3]{1,4,3,2,0:T(4,128)S(1)} fusion(f32[8,128,3,64,3]{1,3,4,2,0:T(8,128)S(1)} %get-tuple-element.36), kind=kOutput, calls=%fused_computation.40 | convolution fusion | flops 21233700 | bytes 4718592 | tf_op jit(solution)/shard_map/jit(fft)/dot.3 | solution.py:23
  22.7 6.8 %add_bitcast_fusion.1 = f32[8,128,3,3,64]{1,3,4,2,0:T(4,128)S(1)} fusion(f32[8,128,3,64,3]{1,4,3,2,0:T(4,128)S(1)} %fusion.30, f32[8,128,3,64,3]{1,3,4,2,0:T(8,128)S(1)} %get-tuple-element.38), kind=kOutput, calls=%fused_computation.46 | convolution fusion | flops 21823532 | bytes 7077888 | tf_op jit(solution)/shard_map/jit(fft)/dot.4 | solution.py:23
  29.5 6.9 %subtract_bitcast_fusion.1 = f32[8,128,3,3,64]{1,3,4,2,0:T(4,128)S(1)} fusion(f32[8,128,3,64,3]{1,4,3,2,0:T(4,128)S(1)} %fusion.30, f32[8,128,3,64,3]{1,3,4,2,0:T(8,128)S(1)} %get-tuple-element.37), kind=kOutput, calls=%fused_computation.47 | convolution fusion | flops 21823532 | bytes 7077888 | tf_op jit(solution)/shard_map/jit(fft)/dot.5 | solution.py:23
  39.0 9.8 %all-to-all-start = ((bf16[8,128,3,2,96]{1,0,3,2,4:T(8,128)(2,1)}), bf16[8,128,3,2,96]{1,0,3,2,4:T(8,128)(2,1)S(1)}, u32[]{:S(2)}, u32[]{:S(2)}) async-start(bf16[8,128,3,2,96]{1,0,3,2,4:T(8,128)(2,1)} %copy.163), calls=%async_computation | async-start | bytes 2359296 | tf_op jit(solution)/shard_map/all_to_all | solution.py:48
  48.8 15.6 %fusion.287 = (f32[96,128,128,1]{2,3,1,0:T(1,128)}, f32[96,128,128,1]{2,3,1,0:T(1,128)}) fusion(f32[96,128,128,2]{2,3,1,0:T(2,128)} %param.12), kind=kLoop, calls=%fused_computation.302 | loop fusion | bytes 25165824 | tf_op jit(solution)/shard_map/slice | solution.py:16
  78.1 7.1 %fusion.96 = bf16[8,128,96,2,3]{1,0,3,4,2:T(8,128)(2,1)S(1)} fusion(bf16[96,128,1,128,2]{3,1,4,2,0:T(8,128)(2,1)} %get-tuple-element.46, bf16[96,128,1,128,2]{3,1,4,2,0:T(8,128)(2,1)} %get-tuple-element.45, bf16[8,128,96,2,3,1]{1,2,3,0,4,5:T(8,128)(2,1)S(1)} %fusion.101), kind=kOutput, calls=%fused_computation.121 | convolution fusion | flops 327745536 | bytes 14942208 | tf_op jit(solution)/shard_map/losir,bilrm->bolsm/dot_general | solution.py:50
  94.6 17.6 %all-to-all-done.1 = bf16[8,128,96,2,3]{1,3,0,4,2:T(2,128)(2,1)S(1)} async-done(((bf16[8,128,96,2,3]{1,3,0,4,2:T(2,128)(2,1)}), bf16[8,128,96,2,3]{1,3,0,4,2:T(2,128)(2,1)S(1)}, u32[]{:S(2)}, u32[]{:S(2)}) %all-to-all-start.1) | async-done | bytes 1179680 | tf_op jit(solution)/shard_map/all_to_all | solution.py:52
  118.3 12.6 %reverse.8 = f32[8,128,3,95]{1,3,2,0:T(8,128)} reverse(f32[8,128,3,95]{1,3,2,0:T(8,128)} %slice.82), dimensions={3} | reverse | bytes 2334720 | tf_op jit(solution)/shard_map/jit(fft)/reverse | solution.py:30
  142.6 6.6 %fusion.22 = f32[8,128,3,64,3]{1,4,3,2,0:T(4,128)S(1)} fusion(f32[8,128,3,64,3]{1,3,4,2,0:T(8,128)S(1)} %get-tuple-element.34), kind=kOutput, calls=%fused_computation.32 | convolution fusion | flops 21233708 | bytes 4718592 | tf_op jit(solution)/shard_map/jit(fft)/dot.10 | solution.py:30
  155.7 7.7 %multiply_bitcast_fusion.1 = f32[8,128,3,3,64]{1,3,4,2,0:T(4,128)S(1)} fusion(f32[8,128,3,64,3]{1,4,3,2,0:T(4,128)S(1)} %fusion.20, f32[8,128,3,64,3]{1,4,3,2,0:T(4,128)S(1)} %fusion.22, f32[8,128,3,64,3]{1,3,4,2,0:T(8,128)S(1)} %get-tuple-element.33), kind=kOutput, calls=%fused_computation.45 | convolution fusion | flops 24182820 | bytes 9437184 | tf_op jit(solution)/shard_map/jit(fft)/dot.9 | solution.py:30
  173.6 6.5 %fusion.18 = f32[8,128,3,64,3]{1,4,3,2,0:T(4,128)S(1)} fusion(f32[8,128,3,64,3]{1,3,4,2,0:T(8,128)S(1)} %get-tuple-element.30), kind=kOutput, calls=%fused_computation.28 | convolution fusion | flops 21233700 | bytes 4718592 | tf_op jit(solution)/shard_map/jit(fft)/dot.3 | solution.py:23
  180.1 7.2 %add_bitcast_fusion = f32[8,128,3,3,64]{1,3,4,2,0:T(4,128)S(1)} fusion(f32[8,128,3,64,3]{1,4,3,2,0:T(4,128)S(1)} %fusion.18, f32[8,128,3,64,3]{1,3,4,2,0:T(8,128)S(1)} %get-tuple-element.32), kind=kOutput, calls=%fused_computation.43 | convolution fusion | flops 21823532 | bytes 7077888 | tf_op jit(solution)/shard_map/jit(fft)/dot.4 | solution.py:23
  187.3 6.9 %subtract_bitcast_fusion = f32[8,128,3,3,64]{1,3,4,2,0:T(4,128)S(1)} fusion(f32[8,128,3,64,3]{1,4,3,2,0:T(4,128)S(1)} %fusion.18, f32[8,128,3,64,3]{1,3,4,2,0:T(8,128)S(1)} %get-tuple-element.31), kind=kOutput, calls=%fused_computation.44 | convolution fusion | flops 21823532 | bytes 7077888 | tf_op jit(solution)/shard_map/jit(fft)/dot.5 | solution.py:23
  196.2 22.9 %all_to_all.68 = bf16[8,128,3,2,96]{1,0,3,2,4:T(8,128)(2,1)S(1)} all-to-all(bf16[8,128,3,2,96]{1,0,3,2,4:T(8,128)(2,1)S(1)} %copy.195), channel_id=1, replica_groups=mesh['member'=1,'lat'=32] {'lat'}, dimensions={4} | all-to-all | bytes 2359296 | tf_op jit(solution)/shard_map/all_to_all | solution.py:56
  220.4 10.2 %convolution_bitcast_fusion = f32[96,128,2,128,2]{3,1,4,2,0:T(8,128)} fusion(bf16[8,128,96,2,3,1]{1,2,3,0,4,5:T(8,128)(2,1)S(1)} %copy-done.7, bf16[8,128,96,2,3,1]{1,2,3,0,4,5:T(8,128)(2,1)S(1)} %fusion.99), kind=kOutput, calls=%fused_computation.6 | convolution fusion | flops 301989888 | bytes 27525120 | tf_op jit(solution)/shard_map/bolsm,bilrm->losir/dot_general | solution.py:58
  239.1 28.7 %all_to_all.69 = bf16[8,128,96,2,3]{1,3,0,4,2:T(2,128)(2,1)S(1)} all-to-all(bf16[8,128,96,2,3]{1,3,0,4,2:T(2,128)(2,1)S(1)} %copy.204), channel_id=1, replica_groups=mesh['member'=1,'lat'=32] {'lat'}, dimensions={2} | all-to-all | bytes 2359296 | tf_op jit(solution)/shard_map/all_to_all | solution.py:62
  270.2 10.0 %reverse.11 = f32[8,128,3,95]{1,3,2,0:T(8,128)S(1)} reverse(f32[8,128,3,95]{1,3,2,0:T(8,128)} %slice.89), dimensions={3} | reverse | bytes 2334720 | tf_op jit(solution)/shard_map/jit(fft)/reverse.1 | solution.py:30
  283.0 12.5 %reverse.10 = f32[8,128,3,95]{1,3,2,0:T(8,128)} reverse(f32[8,128,3,95]{1,3,2,0:T(8,128)} %slice.88), dimensions={3} | reverse | bytes 2334720 | tf_op jit(solution)/shard_map/jit(fft)/reverse | solution.py:30
  307.1 6.7 %fusion.10 = f32[8,128,3,64,3]{1,4,3,2,0:T(4,128)S(1)} fusion(f32[8,128,3,64,3]{1,3,4,2,0:T(8,128)S(1)} %get-tuple-element.28), kind=kOutput, calls=%fused_computation.20 | convolution fusion | flops 21233708 | bytes 4718592 | tf_op jit(solution)/shard_map/jit(fft)/dot.10 | solution.py:30
  320.3 8.2 %multiply_bitcast_fusion = f32[8,128,3,3,64]{1,3,4,2,0:T(4,128)S(1)} fusion(f32[8,128,3,64,3]{1,4,3,2,0:T(4,128)S(1)} %fusion.8, f32[8,128,3,64,3]{1,4,3,2,0:T(4,128)S(1)} %fusion.10, f32[8,128,3,64,3]{1,3,4,2,0:T(8,128)S(1)} %get-tuple-element.27), kind=kOutput, calls=%fused_computation.42 | convolution fusion | flops 24182820 | bytes 9437184 | tf_op jit(solution)/shard_map/jit(fft)/dot.9 | solution.py:30
  331.8 98.1 %all-reduce.7.cloned.1.call-done = f32[96,128,2,128,2]{3,1,4,2,0:T(8,128)} async-done(((f32[96,128,2,128,2]{3,1,4,2,0:T(8,128)}), f32[96,128,2,128,2]{3,1,4,2,0:T(8,128)}) %all-reduce.7.cloned.1.call-update) | async-done | bytes 25165840 | tf_op jit(solution)/shard_map/psum | solution.py:59
  435.9 9.2 %fusion.7 = f32[96,128,128,1]{2,1,0,3:T(8,128)} fusion(f32[96,128,2,128,2]{3,1,4,2,0:T(8,128)} %all-reduce.7.cloned.1.call-done), kind=kLoop, calls=%fused_computation.12 | loop fusion | flops 1572864 | bytes 18874368 | tf_op jit(solution)/shard_map/add | solution.py:64
  445.1 8.9 %pad_maximum_fusion.1 = f32[96,128,128,2]{2,1,0,3:T(8,128)} fusion(f32[96,128,128,1]{2,1,0,3:T(8,128)S(1)} %fusion.5, f32[96,128,128,1]{2,1,0,3:T(8,128)} %fusion.7), kind=kLoop, calls=%fused_computation.1 | loop fusion | flops 3145728 | bytes 25165824 | tf_op jit(solution)/shard_map/stack | solution.py:64
  454.0 22.0 %copy.222 = f32[96,128,128,2]{2,3,1,0:T(2,128)} copy(f32[96,128,128,2]{2,1,0,3:T(8,128)} %pad_maximum_fusion.1) | data formatting | bytes 25165824
  (104 shorter events, 112.7 us)
Async XLA Ops:
  7.2 1.7 copy-start.8
  8.8 3.9 copy-start.1
  39.0 37.4 %all-to-all-start = ((bf16[8,128,3,2,96]{1,0,3,2,4:T(8,128)(2,1)}), bf16[8,128,3,2,96]{1,0,3,2,4:T(8,128)(2,1)S(1)}, u32[]{:S(2)}, u32[]{:S(2)}) async-start(bf16[8,128,3,2,96]{1,0,3,2,4:T(8,128)(2,1)} %copy.163), calls=%async_computation | async-start | bytes 2359296 | tf_op jit(solution)/shard_map/all_to_all | solution.py:48
  65.4 19.8 %copy-start.9 = (bf16[3,96,96]{1,2,0:T(8,128)(2,1)}, bf16[3,96,96]{1,2,0:T(8,128)(2,1)S(1)}, u32[]{:S(2)}) copy-start(bf16[3,96,96]{1,2,0:T(8,128)(2,1)S(1)} %copy.276) | copy-start | bytes 165892
  65.4 4.6 copy-start
  78.0 7.1 %copy-start.6 = (bf16[8,128,96,2,3,1]{1,2,3,0,4,5:T(8,128)(2,1)}, bf16[8,128,96,2,3,1]{1,2,3,0,4,5:T(8,128)(2,1)S(1)}, u32[]{:S(2)}) copy-start(bf16[8,128,96,2,3,1]{1,2,3,0,4,5:T(8,128)(2,1)S(1)} %fusion.101) | copy-start | bytes 3538948
  87.6 24.6 %all-to-all-start.1 = ((bf16[8,128,96,2,3]{1,3,0,4,2:T(2,128)(2,1)}), bf16[8,128,96,2,3]{1,3,0,4,2:T(2,128)(2,1)S(1)}, u32[]{:S(2)}, u32[]{:S(2)}) async-start(bf16[8,128,96,2,3]{1,3,0,4,2:T(2,128)(2,1)} %copy.173), calls=%async_computation.1 | async-start | bytes 2359296 | tf_op jit(solution)/shard_map/all_to_all | solution.py:52
  93.9 336.0 %all-reduce.7.cloned.1.call-start = ((), (), s32[]{:S(2)}) async-start(), calls=%async_computation.4 | async-start | bytes 50331648 | tf_op jit(solution)/shard_map/psum | solution.py:59
  115.5 1.4 copy-start.5
  163.4 1.7 copy-start.3
  167.8 2.5 copy-start.2
  194.5 0.7 copy-start.12
  196.2 23.1 %copy-start.10 = (bf16[3,96,96]{1,2,0:T(8,128)(2,1)S(1)}, bf16[3,96,96]{1,2,0:T(8,128)(2,1)}, u32[]{:S(2)}) copy-start(bf16[3,96,96]{1,2,0:T(8,128)(2,1)} %copy-done.9) | copy-start | bytes 165892
  219.1 1.3 copy-start.7
  267.9 0.6 copy-start.11
  328.5 1.7 copy-start.4
Sparse Core Ops, SparseCore 0:
  230.8 199.0 all-reduce.6
where the time goes:
time: 493 us; the launch traced here: 483 us
  matrix products  140 us (28%)
  waiting for transfers between devices  116 us (24%)
  local copies, waits for them, and re-layouts  99.9 us (20%)
  blocking collectives  51.5 us (10%)
  other arithmetic  44.6 us (9%)
  starting transfers between devices  16.1 us (3%)
  between operations  14.9 us (3%)
    psum x1, waiting for transfers between devices, local_step(): gw_total = lax.psum(gw_part, 'lat')  98.1 us
    another operation x12, matrix products, synthesis(): return jnp.fft.irfft(jnp.pad(complex_spec, pad_width), n=lon_count, axis=-1)  59.1 us
    another operation x11, matrix products, analysis(): spectrum = jnp.fft.rfft(values, axis=-1)[..., :mode_count] * mode_gains  53.8 us
    another operation x12, local copies, waits for them, and re-layouts, synthesis(): return jnp.fft.irfft(jnp.pad(complex_spec, pad_width), n=lon_count, axis=-1)  42.9 us
    unnamed x29, local copies, waits for them, and re-layouts  28.7 us
    all_to_all x1, blocking collectives, local_step(): grad_four_lat = lax.all_to_all(grad_four_own, 'lat', 2, 4, tiled=True)  28.7 us
    all_to_all x1, blocking collectives, local_step(): grad_back_own = lax.all_to_all(grad_back_lat, 'lat', 4, 2, tiled=True)  22.9 us
    all_to_all x1, waiting for transfers between devices, local_step(): back_lat = lax.all_to_all(back_own, 'lat', 2, 4, tiled=True)  17.6 us
  transfers between devices with their start and end apart: 3, of which 2 were waited for; matrix products, arithmetic and copies ran while one was open for 20% of the time, Pallas kernels for 0%

commit v1 on v0

v1 whole, which is shorter than its diff:
```python
import functools
import math
import numpy as np
import jax
import jax.numpy as jnp
from jax import lax
from jax.experimental import pallas as pl
from jax.experimental.pallas import tpu as pltpu
from jax.sharding import PartitionSpec as P

MESH = pl.DeviceIdType.MESH
F32, BF16 = jnp.float32, jnp.bfloat16
VMEM = pltpu.VMEM


class Dims:
    def __init__(self, n, batch, chan, rows, lon):
        self.n = n
        self.side = math.isqrt(n // 2)
        self.b, self.c, self.t, self.lon = batch, chan, rows, lon
        self.lat = n * rows
        self.bt = batch * rows
        self.msg = 2 * rows * self.bt
        self.pitch = self.msg + 8
        self.lp = self.lat + 8
        self.ship_off = [batch * j * (j + 1) for j in range(rows + 1)]


def split_const(mat):
    hi = mat.astype(jnp.bfloat16)
    lo = (mat - hi.astype(np.float64)).astype(jnp.bfloat16)
    return hi, lo


def dft_constants(d):
    m = np.arange(d.lat)
    ang = 2.0 * np.pi * np.outer(m, np.arange(d.lon)) / d.lon
    scale = 1.0 / math.sqrt(d.lon)
    ana = scale * np.concatenate([np.cos(ang), -np.sin(ang)])
    gain = np.where(m == 0, 1.0, 2.0)[:, None]
    ana2 = scale * np.concatenate([np.cos(ang) * gain, -np.sin(ang) * gain])
    syn = ana2.T
    syn2 = ana.T
    return [split_const(a) for a in (ana, ana2, syn, syn2)]


def perm_constant(d):
    t = np.arange(d.lat)
    tau = (t % d.t) * d.n + t // d.t
    mat = np.zeros((d.lat, d.lat))
    mat[t, tau] = 1.0
    return mat.astype(jnp.bfloat16)


def mm(a, b):
    return jnp.dot(a, b, preferred_element_type=F32)


def mm_nt(a, b):
    return lax.dot_general(a, b, (((1,), (1,)), ((), ())), preferred_element_type=F32)


def mm_tn(a, b):
    return lax.dot_general(a, b, (((0,), (0,)), ((), ())), preferred_element_type=F32)


def rnd(x):
    return x.astype(BF16).astype(F32)


def target(d, me, k):
    s = d.side
    y, x, h = me // (2 * s), lax.rem(me // 2, s), lax.rem(me, 2)
    dy, dx, dh = k // (2 * s), lax.rem(k // 2, s), lax.rem(k, 2)
    to = lax.rem(y + dy, s) * (2 * s) + lax.rem(x + dx, s) * 2 + lax.rem(h + dh, 2)
    fro = lax.rem(y - dy + s, s) * (2 * s) + lax.rem(x - dx + s, s) * 2 + lax.rem(h + dh, 2)
    return to, fro


def barrier(d, me):
    sem = pltpu.get_barrier_semaphore()

    def body(k, _):
        pl.semaphore_signal(sem, inc=1, device_id={"lat": lax.rem(me + k, d.n)}, device_id_type=MESH)
        return 0
    lax.fori_loop(1, d.n, body, 0)
    pl.semaphore_wait(sem, d.n - 1)


def send_copy(d, me, k, send, recv, ssem, rsem):
    to, _ = target(d, me, k)
    return pltpu.make_async_remote_copy(
        src_ref=send.at[to], dst_ref=recv.at[me], send_sem=ssem.at[k], recv_sem=rsem.at[k],
        device_id={"lat": to}, device_id_type=MESH)


def exchange(d, me, send, recv, ssem, rsem):
    recv[me] = send[me]

    def start(k, _):
        send_copy(d, me, k, send, recv, ssem, rsem).start()
        return 0

    def wait(k, _):
        send_copy(d, me, k, send, recv, ssem, rsem).wait()
        return 0
    lax.fori_loop(1, d.n, start, 0)
    lax.fori_loop(1, d.n, wait, 0)


def to_messages(d, stage, send):
    def body(s, _):
        send[s] = stage[pl.ds(pl.multiple_of(s * d.pitch, 8), d.msg), :].astype(BF16)
        return 0
    lax.fori_loop(0, d.n, body, 0)


def from_messages(d, recv, stage):
    def body(s, _):
        stage[pl.ds(pl.multiple_of(s * d.pitch, 8), d.msg), :] = recv[s].astype(F32)
        return 0
    lax.fori_loop(0, d.n, body, 0)


def ring_rows(d, start):
    return pl.ds(start, d.n, stride=d.pitch)


def put_modes(d, stage, y, bt, lanes):
    for rk in range(2 * d.t):
        stage[ring_rows(d, rk * d.bt + bt), :] = y[rk * d.n:(rk + 1) * d.n, lanes]


def get_modes(d, stage, bt):
    return jnp.concatenate([stage[ring_rows(d, rk * d.bt + bt), :] for rk in range(2 * d.t)], axis=0)


def analyse(x, hi, lo):
    xh = x.astype(BF16)
    xl = (x - xh.astype(F32)).astype(BF16)
    return mm(hi[...], xh) + mm(lo[...], xh) + mm(hi[...], xl)


def pairs(d, body):
    def step(p, _):
        body(2 * p)
        return 0
    lax.fori_loop(0, d.bt // 2, step, 0)


def lane_halves(d):
    return slice(0, d.c), slice(d.c, 2 * d.c)


def permuted(d, perm, p, out, outt):
    for k in range(d.t):
        pk = p[k].astype(BF16)
        if out is not None:
            out[k] = mm(pk, perm[...]).astype(BF16)
        if outt is not None:
            outt[k] = mm_tn(perm[...], pk.T).astype(BF16)


def spec_rows(d, r, k, b):
    return pl.ds(pl.multiple_of(((r * d.t + k) * d.b + b) * d.lp, 8), d.lat)


def to_spectral(d, stage, spec, p):
    for k in range(d.t):
        def body(b, _):
            x = jnp.concatenate([jnp.concatenate(
                [stage[ring_rows(d, (r * d.t + k) * d.bt + b * d.t + t), :] for t in range(d.t)], axis=0)
                for r in range(2)], axis=1)
            y = rnd(mm(p[k], x.astype(BF16)))
            for r, half in enumerate(lane_halves(d)):
                spec[spec_rows(d, r, k, b), :] = y[:, half]
            return 0
        lax.fori_loop(0, d.b, body, 0)


def from_spectral(d, spec, stage, pt):
    for k in range(d.t):
        def body(b, _):
            x = jnp.concatenate([spec[spec_rows(d, r, k, b), :] for r in range(2)], axis=1).astype(BF16)
            y = mm(pt[k], x)
            for r, half in enumerate(lane_halves(d)):
                for t in range(d.t):
                    stage[ring_rows(d, (r * d.t + k) * d.bt + b * d.t + t), :] = y[t * d.n:(t + 1) * d.n, half]
            return 0
        lax.fori_loop(0, d.b, body, 0)


def mix(d, spec, w, ship, forward):
    half = d.t * d.b * d.lp
    for j in range(d.t):
        rows = d.b * (j + 1)

        def body(ll, _):
            l = d.n * j + ll
            at = [pl.ds(r * half + l, rows, stride=d.lp) for r in range(2)]
            x = jnp.concatenate([spec[at[0], :], spec[at[1], :]], axis=0).astype(BF16)
            ship[ll, d.ship_off[j]:d.ship_off[j + 1], :] = x
            wp = [w[pl.ds(l * 2 * d.c + r, d.c, stride=2), :].astype(BF16) for r in range(2)]
            if forward:
                y = mm_nt(x, jnp.concatenate(wp, axis=0))
                re = y[:rows, :d.c] - y[rows:, d.c:]
                im = y[rows:, :d.c] + y[:rows, d.c:]
            else:
                y = mm(x, jnp.concatenate(wp, axis=1))
                re = y[:rows, :d.c] + y[rows:, d.c:]
                im = y[rows:, :d.c] - y[:rows, d.c:]
            spec[at[0], :] = rnd(re)
            spec[at[1], :] = rnd(im)
            return 0
        lax.fori_loop(0, d.n, body, 0)


def gelu_grad(values):
    cumulative = 0.5 * (1.0 + lax.erf(values * math.sqrt(0.5)))
    density = jnp.exp(-0.5 * values * values) * (1.0 / math.sqrt(2.0 * math.pi))
    return cumulative + values * density


def analysis_kernel(d, f, hi, lo, recv, stage, send, ssem, rsem):
    me = lax.axis_index("lat")
    barrier(d, me)

    def body(bt):
        y = analyse(jnp.concatenate([f[bt], f[bt + 1]], axis=1), hi, lo)
        for u, half in enumerate(lane_halves(d)):
            put_modes(d, stage, y, bt + u, half)
    pairs(d, body)
    to_messages(d, stage, send)
    exchange(d, me, send, recv, ssem, rsem)


def spectral_kernel(d, forward, got, pin, pout, perm, w, recv, ship_recv, stage, spec, send, ship, p, pt, ssem, rsem, ssem2, rsem2):
    me = lax.axis_index("lat")
    barrier(d, me)
    permuted(d, perm, pin, p, None)
    permuted(d, perm, pout, None, pt)
    from_messages(d, got, stage)
    to_spectral(d, stage, spec, p)
    mix(d, spec, w, ship, forward)
    from_spectral(d, spec, stage, pt)
    to_messages(d, stage, send)
    exchange(d, me, send, recv, ssem, rsem)
    exchange(d, me, ship, ship_recv, ssem2, rsem2)


def grid_kernel(d, got, dg, shi, slo, ahi, alo, recv, stage, send, ssem, rsem):
    me = lax.axis_index("lat")
    barrier(d, me)
    from_messages(d, got, stage)

    def body(bt):
        g = jnp.concatenate([get_modes(d, stage, bt), get_modes(d, stage, bt + 1)], axis=1).astype(BF16)
        h = mm(shi[...], g) + mm(slo[...], g)
        u = jnp.concatenate([dg[bt], dg[bt + 1]], axis=1) * gelu_grad(h)
        y = analyse(u, ahi, alo)
        for i, half in enumerate(lane_halves(d)):
            put_modes(d, stage, y, bt + i, half)
    pairs(d, body)
    to_messages(d, stage, send)
    exchange(d, me, send, recv, ssem, rsem)


def weight_kernel(d, a, dq, out):
    for j in range(d.t):
        rows = d.b * (j + 1)
        at = slice(d.ship_off[j], d.ship_off[j + 1])
        aj = a[:, at, :]
        swapped = jnp.concatenate([-aj[:, rows:], aj[:, :rows]], axis=1)
        both = jnp.concatenate([aj, swapped], axis=2).reshape(d.n * 2 * rows, 2 * d.c)
        y = mm_tn(dq[:, at, :].reshape(d.n * 2 * rows, d.c), both)
        for r, half in enumerate(lane_halves(d)):
            out[pl.ds(j * 2 * d.c + r, d.c, stride=2), :] = y[:, half]


def final_kernel(d, got, dg, shi, slo, out, stage):
    from_messages(d, got, stage)

    def body(bt):
        g = jnp.concatenate([get_modes(d, stage, bt), get_modes(d, stage, bt + 1)], axis=1).astype(BF16)
        y = mm(shi[...], g) + mm(slo[...], g)
        for i, half in enumerate(lane_halves(d)):
            out[bt + i] = dg[bt + i] + y[:, half]
    pairs(d, body)


def call(name, kernel, outs, scratch, args, cid=None):
    single = not isinstance(outs, (list, tuple))
    spec = pl.BlockSpec(memory_space=VMEM)
    params = dict(vmem_limit_bytes=60 * 1024 * 1024)
    if cid is not None:
        params.update(collective_id=cid, has_side_effects=True)
    return pl.pallas_call(
        kernel, name=name, out_shape=outs, in_specs=[spec] * len(args),
        out_specs=spec if single else [spec] * len(outs), scratch_shapes=scratch,
        compiler_params=pltpu.CompilerParams(**params))(*args)


def solution(mesh):
    n = mesh.shape['lat']
    field_spec = P('member', None, 'lat', None)

    def local_step(field_loc, grad_loc, p_fwd, p_inv, w_mix):
        batch, chan, rows, lon = field_loc.shape
        d = Dims(n, batch, chan, rows, lon)
        (ah, al), (bh, bl), (sh, sl), (zh, zl) = dft_constants(d)
        perm = perm_constant(d)
        me = lax.axis_index('lat')
        f = field_loc.transpose(0, 2, 3, 1).reshape(d.bt, lon, chan)
        dg = grad_loc.transpose(0, 2, 3, 1).reshape(d.bt, lon, chan)
        w = w_mix.transpose(0, 1, 3, 2).reshape(-1, chan)
        own = lambda p: lax.dynamic_index_in_dim(p.reshape(d.t, n, d.lat, d.lat), me, 1, False)
        pw, pi = own(p_fwd), own(p_inv)

        msgs = jax.ShapeDtypeStruct((n, d.msg, chan), BF16)
        ships = jax.ShapeDtypeStruct((n, d.ship_off[-1], chan), BF16)
        stage = VMEM((n * d.pitch, chan), F32)
        spec = VMEM((2 * d.t * d.b * d.lp, chan), F32)
        mat = VMEM((d.t, d.lat, d.lat), BF16)
        dma = pltpu.SemaphoreType.DMA((n,))
        sems = [dma, dma]
        buf = lambda s: VMEM(s.shape, s.dtype)

        r1 = call("ana", functools.partial(analysis_kernel, d), msgs, [stage, buf(msgs)] + sems, [f, ah, al], 0)
        spec_scratch = [stage, spec, buf(msgs), buf(ships), mat, mat] + sems + sems
        r2, ship_a = call("fwd", functools.partial(spectral_kernel, d, True), [msgs, ships], spec_scratch, [r1, pw, pi, perm, w], 1)
        r3 = call("grid", functools.partial(grid_kernel, d), msgs, [stage, buf(msgs)] + sems, [r2, dg, sh, sl, bh, bl], 2)
        r4, ship_q = call("bwd", functools.partial(spectral_kernel, d, False), [msgs, ships], spec_scratch, [r3, pi, pw, perm, w], 3)
        dw = call("wgt", functools.partial(weight_kernel, d), jax.ShapeDtypeStruct((d.t * 2 * chan, chan), F32), [], [ship_a, ship_q])
        gathered = lax.all_gather(dw.reshape(d.t, 1, 2 * chan, chan), 'lat', axis=1, tiled=True)
        df = call("fin", functools.partial(final_kernel, d), jax.ShapeDtypeStruct((d.bt, lon, chan), F32), [stage], [r4, dg, zh, zl])
        grad_field = df.reshape(batch, rows, lon, chan).transpose(0, 3, 1, 2)
        grad_wmix = gathered.reshape(d.lat, chan, 2, chan).transpose(0, 1, 3, 2)
        return grad_field, grad_wmix

    return jax.shard_map(local_step, mesh=mesh, in_specs=(field_spec, field_spec, P(), P(), P()), out_specs=(field_spec, P('member', None, None, None)), check_vma=False)
```

time: 493 us -> 307 us (0.62); the launches traced: 483 us -> 307 us
  Pallas kernels: 0 us -> 202 us
  matrix products: 140 us -> 0 us
  local copies, waits for them, and re-layouts: 99.9 us -> 36.7 us
  waiting for transfers between devices: 116 us -> 53.5 us
  blocking collectives: 51.5 us -> 0 us
  other arithmetic: 44.6 us -> 0 us
  starting transfers between devices: 16.1 us -> 0.06 us
    pallas_call x0 -> x6, Pallas kernels: none -> 202 us  [call(): pl.pallas_call(kernel, name=name, out_shape=outs, in_specs=[spec] * len(a...]
    another operation x23 -> x0, matrix products: 113 us -> none  [the longest x12 59.1 us: synthesis(): return jnp.fft.irfft(jnp.pad(complex_spec, pad_width), n=lon_count, axis=-1)]
    psum x1 -> x0, waiting for transfers between devices: 98.1 us -> none  [local_step(): gw_total = lax.psum(gw_part, 'lat')]
    all_gather x0 -> x1, waiting for transfers between devices: none -> 53.5 us  [local_step(): lax.all_gather(dw.reshape(d.t, 1, 2 * chan, chan), 'lat', axis=1, tiled=T...]
    all_to_all x2 -> x0, blocking collectives: 51.5 us -> none  [the longest x1 28.7 us: local_step(): grad_four_lat = lax.all_to_all(grad_four_own, 'lat', 2, 4, tiled=True)]
    another operation x18 -> x0, local copies, waits for them, and re-layouts: 46.1 us -> none  [the longest x12 42.9 us: synthesis(): return jnp.fft.irfft(jnp.pad(complex_spec, pad_width), n=lon_count, axis=-1)]
    dot_general x7 -> x0, matrix products: 27.2 us -> none  [the longest x1 10.2 us: local_step(): jnp.einsum('bolsm,bilrm->losir', grad_mixed, coeffs, preferred_element_ty...]
    another operation x17 -> x0, other arithmetic: 21 us -> none  [the longest x1 8.92 us: local_step(): jnp.stack([gw_total[:, :, 0, :, 0] + gw_total[:, :, 1, :, 1], gw_total[:,...]
  transfers between devices with their start and end apart: 3 -> 1, of which waited for: 2 -> 1; matrix products, arithmetic and copies ran while one was open for 20% -> 0% of each run, Pallas kernels for 0% -> 2%
where the time goes in v1:
time: 307 us
  Pallas kernels  202 us (66%)
  waiting for transfers between devices  53.5 us (17%)
  local copies, waits for them, and re-layouts  36.7 us (12%)
  between operations  14.1 us (5%)
    pallas_call x6, Pallas kernels, call(): pl.pallas_call(kernel, name=name, out_shape=outs, in_specs=[spec] * len(a...  202 us
    all_gather x1, waiting for transfers between devices, local_step(): lax.all_gather(dw.reshape(d.t, 1, 2 * chan, chan), 'lat', axis=1, tiled=T...  53.5 us
    unnamed x1, local copies, waits for them, and re-layouts  18.6 us
    all_gather x1, local copies, waits for them, and re-layouts, local_step(): lax.all_gather(dw.reshape(d.t, 1, 2 * chan, chan), 'lat', axis=1, tiled=T...  16.3 us
  transfers between devices with their start and end apart: 1, of which 1 were waited for; matrix products, arithmetic and copies ran while one was open for 0% of the time, Pallas kernels for 2%

profile of v1, /device:TPU:97, one launch (start us, length us, event | category | flops | bytes accessed | tf_op | source)
XLA Modules:
  0.0 306.6 jit_solution(15266975118052869512)
XLA Ops:
  7.2 0.1 all-gather.2.cloned.1.call-start
  7.2 1.7 dynamic-slice_bitcast_fusion
  9.0 32.9 %ana.1.got = bf16[32,144,128]{2,1,0:T(8,128)(2,1)} custom-call(f32[24,192,128]{2,1,0:T(8,128)} %bitcast.31, bf16[192,192]{1,0:T(8,128)(2,1)} %constant.30.clone.hi, bf16[192,192]{1,0:T(8,128)(2,1)} %constant.31.clone.lo), custom_call_target="tpu_custom_call" | custom-call | tf_op jit(solution)/shard_map/ana/pallas_call | solution.py:297
  41.9 64.2 %fwd.1 = (bf16[32,144,128]{2,1,0:T(8,128)(2,1)}, bf16[32,96,128]{2,1,0:T(8,128)(2,1)}) custom-call(bf16[32,144,128]{2,1,0:T(8,128)(2,1)} %ana.1.got, f32[3,96,96]{2,1,0:T(8,128)} %get-tuple-element.13.pin.pout, f32[3,96,96]{2,1,0:T(8,128)} %get-tuple-element.12.pout.pin, bf16[96,96]{1,0:T(8,128)(2,1)} %constant.32.clone.perm, f32[24576,128]{1,0:T(8,128)} %bitcast.27), custom_call_target="tpu_custom_call" | custom-call | tf_op jit(solution)/shard_map/fwd/pallas_call | solution.py:297
  106.1 33.4 %grid.1.got = bf16[32,144,128]{2,1,0:T(8,128)(2,1)} custom-call(bf16[32,144,128]{2,1,0:T(8,128)(2,1)} %get-tuple-element.6.got, f32[24,192,128]{2,1,0:T(8,128)} %bitcast.29, bf16[192,192]{1,0:T(8,128)(2,1)} %constant.33.clone.shi, bf16[192,192]{1,0:T(8,128)(2,1)} %constant.34.clone.slo, bf16[192,192]{1,0:T(8,128)(2,1)} %constant.35.clone.ahi, ...), custom_call_target="tpu_custom_call" | custom-call | tf_op jit(solution)/shard_map/grid/pallas_call | solution.py:297
  139.5 63.1 %bwd.1 = (bf16[32,144,128]{2,1,0:T(8,128)(2,1)}, bf16[32,96,128]{2,1,0:T(8,128)(2,1)}) custom-call(bf16[32,144,128]{2,1,0:T(8,128)(2,1)} %grid.1.got, f32[3,96,96]{2,1,0:T(8,128)} %get-tuple-element.12.pout.pin, f32[3,96,96]{2,1,0:T(8,128)} %get-tuple-element.13.pin.pout, bf16[96,96]{1,0:T(8,128)(2,1)} %constant.32.clone.perm, f32[24576,128]{1,0:T(8,128)} %bitcast.28), custom_call_target="tpu_custom_call" | custom-call | tf_op jit(solution)/shard_map/bwd/pallas_call | solution.py:297
  202.6 2.5 wgt.1
  205.1 0.1 all-gather.2.cloned.1.call-update
  205.2 6.1 %fin.1 = f32[24,192,128]{2,1,0:T(8,128)} custom-call(bf16[32,144,128]{2,1,0:T(8,128)(2,1)} %get-tuple-element.7.got, f32[24,192,128]{2,1,0:T(8,128)} %bitcast.30, bf16[192,192]{1,0:T(8,128)(2,1)} %constant.37.clone.shi, bf16[192,192]{1,0:T(8,128)(2,1)} %constant.38.clone.slo), custom_call_target="tpu_custom_call" | custom-call | tf_op jit(solution)/shard_map/fin/pallas_call | solution.py:297
  211.3 53.5 %all-gather.2.cloned.1.call-done = f32[3,32,256,128]{3,2,0,1:T(8,128)} async-done(((f32[3,1,256,128]{3,2,0,1:T(8,128)}), f32[3,32,256,128]{3,2,0,1:T(8,128)}) %all-gather.2.cloned.1.call-update) | async-done | bytes 12582928 | tf_op jit(solution)/shard_map/all_gather | solution.py:334
  264.8 16.3 %copy.23 = f32[3,32,256,128]{3,1,0,2:T(8,128)} copy(f32[3,32,256,128]{3,2,0,1:T(8,128)} %all-gather.2.cloned.1.call-done) | data formatting | bytes 25165824 | tf_op jit(solution)/shard_map/all_gather | solution.py:334
  281.1 18.6 %copy.24 = f32[96,128,128,2]{2,3,1,0:T(2,128)} copy(f32[96,128,128,2]{2,0,3,1:T(8,128)} %bitcast.26) | data formatting | bytes 25165824
Async XLA Ops:
  7.2 257.6 %all-gather.2.cloned.1.call-start = ((), (), s32[]{:S(2)}) async-start(), calls=%async_computation | async-start | bytes 12976128 | tf_op jit(solution)/shard_map/all_gather | solution.py:334
Sparse Core Ops, SparseCore 0:
  205.3 59.4 all-gather.1

commit v2 on v1

v2 whole, which is shorter than its diff:
```python
import functools
import math
import numpy as np
import jax
import jax.numpy as jnp
from jax import lax
from jax.experimental import pallas as pl
from jax.experimental.pallas import tpu as pltpu
from jax.sharding import PartitionSpec as P

MESH = pl.DeviceIdType.MESH
F32, BF16 = jnp.float32, jnp.bfloat16
VMEM = pltpu.VMEM


class Dims:
    def __init__(self, n, batch, chan, rows, lon):
        self.n = n
        self.side = math.isqrt(n // 2)
        self.b, self.c, self.t, self.lon = batch, chan, rows, lon
        self.lat = n * rows
        self.bt = batch * rows
        self.msg = 2 * rows * self.bt
        self.pitch = self.msg + 8
        self.lp = self.lat + 8
        self.ship_off = [batch * j * (j + 1) for j in range(rows + 1)]


def split_const(mat):
    hi = mat.astype(jnp.bfloat16)
    lo = (mat - hi.astype(np.float64)).astype(jnp.bfloat16)
    return hi, lo


def dft_constants(d):
    m = np.arange(d.lat)
    ang = 2.0 * np.pi * np.outer(m, np.arange(d.lon)) / d.lon
    scale = 1.0 / math.sqrt(d.lon)
    ana = scale * np.concatenate([np.cos(ang), -np.sin(ang)])
    gain = np.where(m == 0, 1.0, 2.0)[:, None]
    ana2 = scale * np.concatenate([np.cos(ang) * gain, -np.sin(ang) * gain])
    syn = ana2.T
    syn2 = ana.T
    return [split_const(a) for a in (ana, ana2, syn, syn2)]


def perm_constant(d):
    t = np.arange(d.lat)
    tau = (t % d.t) * d.n + t // d.t
    mat = np.zeros((d.lat, d.lat))
    mat[t, tau] = 1.0
    return mat.astype(jnp.bfloat16)


def mm(a, b):
    return jnp.dot(a, b, preferred_element_type=F32)


def mm_nt(a, b):
    return lax.dot_general(a, b, (((1,), (1,)), ((), ())), preferred_element_type=F32)


def mm_tn(a, b):
    return lax.dot_general(a, b, (((0,), (0,)), ((), ())), preferred_element_type=F32)


def rnd(x):
    return x.astype(BF16).astype(F32)


def place(d, me):
    return me // (2 * d.side), lax.rem(me // 2, d.side), lax.rem(me, 2)


def shifted(d, me, dy, dx, dh):
    y, x, h = place(d, me)
    s = d.side
    return (lax.rem(y + dy + 2 * s, s) * s + lax.rem(x + dx + 2 * s, s)) * 2 + lax.rem(h + dh, 2)


def remote(src, dst, ssem, rsem, to):
    return pltpu.make_async_remote_copy(src_ref=src, dst_ref=dst, send_sem=ssem, recv_sem=rsem,
                                        device_id={"lat": to}, device_id_type=MESH)


def barrier(d, me):
    sem = pltpu.get_barrier_semaphore()

    def body(k, _):
        pl.semaphore_signal(sem, inc=1, device_id={"lat": lax.rem(me + k, d.n)}, device_id_type=MESH)
        return 0
    lax.fori_loop(1, d.n, body, 0)
    pl.semaphore_wait(sem, d.n - 1)


class Exchange:
    def __init__(self, d, me, send, recv, hold, ssem, rsem, hsem, hrecv, fsem):
        self.d, self.me, self.send, self.recv, self.hold = d, me, send, recv, hold
        self.ssem, self.rsem, self.hsem, self.hrecv, self.fsem = ssem, rsem, hsem, hrecv, fsem
        half = d.side // 2
        self.relayed = [(dy, dx) for dy in range(d.side) for dx in range(d.side) if half in (dy, dx)]
        self.half = half

    def key(self, dy, dx, dh):
        return (dy * self.d.side + dx) * 2 + dh

    def direct(self, dy, dx, dh):
        k = self.key(dy, dx, dh)
        to = shifted(self.d, self.me, dy, dx, dh)
        return to, remote(self.send.at[to], self.recv.at[self.me], self.ssem.at[k], self.rsem.at[k], to)

    def hop(self, dy, dx):
        return -int(dy == self.half), -int(dx == self.half)

    def relay_out(self, i):
        dy, dx = self.relayed[i]
        ry, rx = self.hop(dy, dx)
        to = shifted(self.d, self.me, dy, dx, 1)
        via = shifted(self.d, self.me, ry, rx, 0)
        return to, remote(self.send.at[to], self.hold.at[i], self.hsem.at[i], self.hrecv.at[i], via)

    def relay_on(self, i):
        dy, dx = self.relayed[i]
        ry, rx = self.hop(dy, dx)
        origin = shifted(self.d, self.me, -ry, -rx, 0)
        to = shifted(self.d, origin, dy, dx, 1)
        return remote(self.hold.at[i], self.recv.at[origin], self.fsem.at[i], self.rsem.at[self.key(dy, dx, 1)], to)

    def directs(self, body):
        s, half = self.d.side, self.half

        def even(i, _):
            body((i + 1) // s, lax.rem(i + 1, s), 0)
            return 0
        lax.fori_loop(0, s * s - 1, even, 0)

        def odd(i, _):
            a, b = i // (s - 1), lax.rem(i, s - 1)
            body(a + a // half, b + b // half, 1)
            return 0
        lax.fori_loop(0, (s - 1) * (s - 1), odd, 0)

    def dispatch(self, fill):
        for i in range(len(self.relayed)):
            to, copy = self.relay_out(i)
            fill(to)
            copy.start()

        def body(dy, dx, dh):
            to, copy = self.direct(dy, dx, dh)
            fill(to)
            copy.start()
        self.directs(body)
        fill(self.me)

    def forward(self):
        for i in range(len(self.relayed)):
            self.relay_out(i)[1].wait_recv()
            self.relay_on(i).start()

    def collect(self, take):
        take(self.me, self.send)

        def body(dy, dx, dh):
            self.direct(dy, dx, dh)[1].wait_recv()
            take(shifted(self.d, self.me, -dy, -dx, dh), self.recv)
        self.directs(body)
        for dy, dx in self.relayed:
            self.direct(dy, dx, 1)[1].wait_recv()
            take(shifted(self.d, self.me, -dy, -dx, 1), self.recv)

    def drain(self):
        self.directs(lambda dy, dx, dh: self.direct(dy, dx, dh)[1].wait_send())
        for i in range(len(self.relayed)):
            self.relay_out(i)[1].wait_send()
            self.relay_on(i).wait_send()


def message_rows(d, s):
    return pl.ds(pl.multiple_of(s * d.pitch, 8), d.msg)


def ring_rows(d, start):
    return pl.ds(start, d.n, stride=d.pitch)


def put_modes(d, stage, y, bt, lanes):
    for rk in range(2 * d.t):
        stage[ring_rows(d, rk * d.bt + bt), :] = y[rk * d.n:(rk + 1) * d.n, lanes]


def get_modes(d, stage, bt):
    return jnp.concatenate([stage[ring_rows(d, rk * d.bt + bt), :] for rk in range(2 * d.t)], axis=0)


def analyse(x, hi, lo):
    xh = x.astype(BF16)
    xl = (x - xh.astype(F32)).astype(BF16)
    return mm(hi[...], xh) + mm(lo[...], xh) + mm(hi[...], xl)


def loop(count, body, unroll=1):
    def step(i, _):
        body(i)
        return 0
    lax.fori_loop(0, count, step, 0, unroll=unroll)


def lane_halves(d):
    return slice(0, d.c), slice(d.c, 2 * d.c)


def permuted(d, perm, p, out, outt):
    for k in range(d.t):
        pk = p[k].astype(BF16)
        out[k] = mm(pk, perm[...]).astype(BF16)
        outt[k] = mm_tn(perm[...], pk.T).astype(BF16)


def to_spectral(d, stage, spec, p):
    for k in range(d.t):
        low = d.n * k

        def body(b):
            x = jnp.concatenate([jnp.concatenate(
                [stage[ring_rows(d, (r * d.t + k) * d.bt + b * d.t + t), :] for t in range(d.t)], axis=0)
                for r in range(2)], axis=1)
            y = rnd(mm(p[k, low:, :], x.astype(BF16)))
            for r, half in enumerate(lane_halves(d)):
                at = pl.multiple_of(((r * d.t + k) * d.b + b) * d.lp + low, 8)
                spec[pl.ds(at, d.lat - low), :] = y[:, half]
        loop(d.b, body, 4)


def from_spectral(d, spec, stage, pt):
    for k in range(d.t):
        low = d.n * k

        def body(b):
            at = [pl.multiple_of(((r * d.t + k) * d.b + b) * d.lp + low, 8) for r in range(2)]
            x = jnp.concatenate([spec[pl.ds(a, d.lat - low), :] for a in at], axis=1).astype(BF16)
            y = mm(pt[k][:, low:], x)
            for r, half in enumerate(lane_halves(d)):
                for t in range(d.t):
                    stage[ring_rows(d, (r * d.t + k) * d.bt + b * d.t + t), :] = y[t * d.n:(t + 1) * d.n, half]
        loop(d.b, body, 4)


def mix(d, spec, out, w, ship, forward):
    half = d.t * d.b * d.lp
    for j in range(d.t):
        rows = d.b * (j + 1)

        def body(ll):
            l = d.n * j + ll
            at = [pl.ds(r * half + l, rows, stride=d.lp) for r in range(2)]
            x = jnp.concatenate([spec[at[0], :], spec[at[1], :]], axis=0).astype(BF16)
            ship[ll, d.ship_off[j]:d.ship_off[j + 1], :] = x
            wp = [w[pl.ds(l * 2 * d.c + r, d.c, stride=2), :].astype(BF16) for r in range(2)]
            if forward:
                y = mm_nt(x, jnp.concatenate(wp, axis=0))
                re = y[:rows, :d.c] - y[rows:, d.c:]
                im = y[rows:, :d.c] + y[:rows, d.c:]
            else:
                y = mm(x, jnp.concatenate(wp, axis=1))
                re = y[:rows, :d.c] + y[rows:, d.c:]
                im = y[rows:, :d.c] - y[:rows, d.c:]
            out[at[0], :] = rnd(re)
            out[at[1], :] = rnd(im)
        loop(d.n, body, 4)


def gelu_grad(values):
    cumulative = 0.5 * (1.0 + lax.erf(values * math.sqrt(0.5)))
    density = jnp.exp(-0.5 * values * values) * (1.0 / math.sqrt(2.0 * math.pi))
    return cumulative + values * density


def weights(d, a, dq, out, me):
    for j in range(d.t):
        rows = d.b * (j + 1)
        at = slice(d.ship_off[j], d.ship_off[j + 1])
        aj = a[:, at, :]
        swapped = jnp.concatenate([-aj[:, rows:], aj[:, :rows]], axis=1)
        both = jnp.concatenate([aj, swapped], axis=2).reshape(d.n * 2 * rows, 2 * d.c)
        y = mm_tn(dq[:, at, :].reshape(d.n * 2 * rows, d.c), both)
        for r, half in enumerate(lane_halves(d)):
            out[j, me, pl.ds(r, d.c, stride=2), :] = y[:, half]


class Gather:
    def __init__(self, d, me, full, s1, r1, s2, r2, sp, rp):
        self.d, self.me, self.full = d, me, full
        self.s1, self.r1, self.s2, self.r2, self.sp, self.rp = s1, r1, s2, r2, sp, rp
        self.h = lax.rem(me, 2)
        self.half = full.shape[2] // 2
        self.sent = []

    def near(self, dev, first, second):
        h = self.h
        return shifted(self.d, dev, first * h + second * (1 - h), first * (1 - h) + second * h, 0)

    def piece(self, block, part):
        if part is None:
            return self.full.at[:, block]
        return self.full.at[:, block, self.half * part:self.half * (part + 1), :]

    def copy(self, block, part, ssem, rsem, to):
        ref = self.piece(block, part)
        return remote(ref, ref, ssem, rsem, to)

    def start(self, *args):
        c = self.copy(*args)
        c.start()
        self.sent.append(c)

    def arrive(self, block, part, rsem):
        self.copy(block, part, self.sp.at[0], rsem, self.partner).wait_recv()

    def run(self, between):
        me, near, s1, r1, s2, r2, sp, rp = self.me, self.near, self.s1, self.r1, self.s2, self.r2, self.sp, self.rp
        p1, m1, o1 = near(me, 1, 0), near(me, -1, 0), near(me, 2, 0)
        p2, m2 = near(me, 0, 1), near(me, 0, -1)
        self.partner = shifted(self.d, me, 0, 0, 1)
        group = [me, m1, p1, o1]

        def second(q):
            self.start(group[q], None, s2.at[q, 0], r2.at[q, 0], p2)
            self.start(group[q], None, s2.at[q, 1], r2.at[q, 1], m2)
            self.start(group[q], None, sp.at[q], rp.at[q], self.partner)

        def relay(q):
            for i, (off, to) in enumerate(((-1, p2), (1, m2))):
                block = near(group[q], 0, off)
                self.arrive(block, None, r2.at[q, i])
                self.start(block, i, s2.at[q, 2 + i], r2.at[q, 2 + i], to)
                self.start(block, None, sp.at[4 + 2 * q + i], rp.at[4 + 2 * q + i], self.partner)

        self.start(me, None, s1.at[0], r1.at[0], p1)
        self.start(me, None, s1.at[1], r1.at[1], m1)
        second(0)
        between()
        self.arrive(m1, None, r1.at[0])
        self.start(m1, 0, s1.at[2], r1.at[2], p1)
        second(1)
        self.arrive(p1, None, r1.at[1])
        self.start(p1, 1, s1.at[3], r1.at[3], m1)
        second(2)
        relay(0)
        self.arrive(o1, 0, r1.at[2])
        self.arrive(o1, 1, r1.at[3])
        second(3)
        for q in (1, 2, 3):
            relay(q)
        for q in range(4):
            block = near(group[q], 0, 2)
            for i in range(2):
                self.arrive(block, i, r2.at[q, 2 + i])
            self.start(block, None, sp.at[12 + q], rp.at[12 + q], self.partner)
        for i in range(16):
            self.arrive(self.partner, None, rp.at[i])
        for c in self.sent:
            c.wait_send()


def main_kernel(d, f_h, dg_h, w_h, pf_h, pi_h, perm, ah, al, bh, bl, sh, sl, recv4, full,
                f, dg, w, pf, pi, pw, pwt, pv, pvt, stage, stage2, spec, spec2, send, recv, hold, ship, shipr, shold,
                isem, ssem, rsem, hsem, hrecv, fsem, s1, r1, s2, r2, sp, rp):
    me = lax.axis_index("lat")
    step = 6
    loads = [pltpu.make_async_copy(f_h.at[i:i + step], f.at[i:i + step], isem.at[i // step]) for i in range(0, d.bt, step)]
    nf = len(loads)
    rest = []
    for k in range(d.t):
        rest.append(pltpu.make_async_copy(pf_h.at[me + k * d.n], pf.at[k], isem.at[nf + 2 * k]))
        rest.append(pltpu.make_async_copy(pi_h.at[me + k * d.n], pi.at[k], isem.at[nf + 2 * k + 1]))
    wload = pltpu.make_async_copy(w_h, w, isem.at[nf + 6])
    gload = pltpu.make_async_copy(dg_h, dg, isem.at[nf + 7])
    for c in loads + rest + [wload, gload]:
        c.start()
    barrier(d, me)

    def exchange(e, snd, rcv, hld):
        return Exchange(d, me, snd, rcv, hld, ssem.at[e], rsem.at[e], hsem.at[e], hrecv.at[e], fsem.at[e])

    ex = [exchange(i, send.at[i], recv.at[i] if i < 3 else recv4, hold.at[i]) for i in range(4)]
    ships = [exchange(4 + i, ship.at[i], shipr.at[i], shold.at[i]) for i in range(2)]

    def fill(e, st):
        def go(s):
            send[e, s] = st[message_rows(d, s), :].astype(BF16)
        return go

    def take(st):
        def go(s, ref):
            st[message_rows(d, s), :] = ref[s].astype(F32)
        return go

    none = lambda *a: None

    for c in range(nf):
        loads[c].wait()

        def analysis_step(p):
            bt = c * step + 2 * p
            y = analyse(jnp.concatenate([f[bt], f[bt + 1]], axis=1), ah, al)
            for u, half in enumerate(lane_halves(d)):
                put_modes(d, stage, y, bt + u, half)
        loop(step // 2, analysis_step, 3)
    ex[0].dispatch(fill(0, stage))
    for c in rest:
        c.wait()
    permuted(d, perm, pf, pw, pwt)
    permuted(d, perm, pi, pv, pvt)
    ex[0].forward()
    ex[0].collect(take(stage2))
    to_spectral(d, stage2, spec, pw)
    wload.wait()
    mix(d, spec, spec2, w, ship.at[0], True)
    from_spectral(d, spec2, stage, pvt)
    ex[1].dispatch(fill(1, stage))
    ships[0].dispatch(none)
    gload.wait()
    ex[1].forward()
    ex[1].collect(take(stage2))

    def grid_step(p):
        bt = 2 * p
        g = jnp.concatenate([get_modes(d, stage2, bt), get_modes(d, stage2, bt + 1)], axis=1).astype(BF16)
        h = mm(sh[...], g) + mm(sl[...], g)
        u = jnp.concatenate([dg[bt], dg[bt + 1]], axis=1) * gelu_grad(h)
        y = analyse(u, bh, bl)
        for i, half in enumerate(lane_halves(d)):
            put_modes(d, stage, y, bt + i, half)
    loop(d.bt // 2, grid_step, 2)
    ex[2].dispatch(fill(2, stage))
    ships[0].forward()
    ex[2].forward()
    ex[2].collect(take(stage2))
    to_spectral(d, stage2, spec, pv)
    mix(d, spec, spec2, w, ship.at[1], False)
    ships[1].dispatch(none)
    from_spectral(d, spec2, stage, pwt)
    ex[3].dispatch(fill(3, stage))
    recv4[me] = send[3, me]

    def ship_take(i):
        def go(s, ref):
            @pl.when(s == me)
            def _():
                shipr[i, s] = ship[i, s]
        return go
    ships[0].collect(ship_take(0))
    ships[1].forward()
    ships[1].collect(ship_take(1))
    weights(d, shipr.at[0], shipr.at[1], full, me)
    gather = Gather(d, me, full, s1, r1, s2, r2, sp, rp)
    gather.run(ex[3].forward)
    ex[3].collect(none)
    for e in ex + ships:
        e.drain()


def final_kernel(d, got, dg_h, full, shi, slo, out, dw, dg, stage, sem):
    copy = pltpu.make_async_copy(full, dw, sem.at[0])
    load = pltpu.make_async_copy(dg_h, dg, sem.at[1])
    copy.start()
    load.start()

    def take(s):
        stage[message_rows(d, s), :] = got[s].astype(F32)
    loop(d.n, take, 2)
    load.wait()

    def body(p):
        bt = 2 * p
        g = jnp.concatenate([get_modes(d, stage, bt), get_modes(d, stage, bt + 1)], axis=1).astype(BF16)
        y = mm(shi[...], g) + mm(slo[...], g)
        for i, half in enumerate(lane_halves(d)):
            out[bt + i] = dg[bt + i] + y[:, half]
    loop(d.bt // 2, body, 2)
    copy.wait()


def solution(mesh):
    n = mesh.shape['lat']
    field_spec = P('member', None, 'lat', None)

    def local_step(field_loc, grad_loc, p_fwd, p_inv, w_mix):
        batch, chan, rows, lon = field_loc.shape
        d = Dims(n, batch, chan, rows, lon)
        (ah, al), (bh, bl), (sh, sl), (zh, zl) = dft_constants(d)
        perm = perm_constant(d)
        f = field_loc.transpose(0, 2, 3, 1).reshape(d.bt, lon, chan)
        dg = grad_loc.transpose(0, 2, 3, 1).reshape(d.bt, lon, chan)
        w = w_mix.transpose(0, 1, 3, 2).reshape(-1, chan)

        nr = 2 * d.side - 1
        sl_rows = d.ship_off[-1]
        stage = VMEM((n * d.pitch, chan), F32)
        spec = VMEM((2 * rows * batch * d.lp, chan), F32)
        mat = VMEM((rows, d.lat, d.lat), BF16)
        raw = VMEM((rows, d.lat, d.lat), F32)
        field = VMEM((d.bt, lon, chan), F32)
        dma = lambda *s: pltpu.SemaphoreType.DMA(s)
        vspec = pl.BlockSpec(memory_space=VMEM)
        aspec = pl.BlockSpec(memory_space=pl.ANY)
        recv4, full = pl.pallas_call(
            functools.partial(main_kernel, d), name="main",
            out_shape=[VMEM((n, d.msg, chan), BF16), VMEM((rows, n, 2 * chan, chan), F32)],
            in_specs=[aspec] * 5 + [vspec] * 7,
            out_specs=[vspec, vspec],
            scratch_shapes=[field, field, VMEM(w.shape, F32), raw, raw, mat, mat, mat, mat, stage, stage, spec, spec,
                            VMEM((4, n, d.msg, chan), BF16), VMEM((3, n, d.msg, chan), BF16), VMEM((4, nr, d.msg, chan), BF16),
                            VMEM((2, n, sl_rows, chan), BF16), VMEM((2, n, sl_rows, chan), BF16), VMEM((2, nr, sl_rows, chan), BF16),
                            dma(12), dma(6, n), dma(6, n), dma(6, nr), dma(6, nr), dma(6, nr),
                            dma(4), dma(4), dma(4, 4), dma(4, 4), dma(16), dma(16)],
            compiler_params=pltpu.CompilerParams(collective_id=0, has_side_effects=True, vmem_limit_bytes=44 * 1024 * 1024),
        )(f, dg, w, p_fwd, p_inv, perm, ah, al, bh, bl, sh, sl)
        df, dw = pl.pallas_call(
            functools.partial(final_kernel, d), name="final",
            out_shape=[jax.ShapeDtypeStruct((d.bt, lon, chan), F32), jax.ShapeDtypeStruct(full.shape, F32)],
            in_specs=[vspec, aspec, vspec, vspec, vspec], out_specs=[vspec, aspec],
            scratch_shapes=[field, stage, dma(2)],
            compiler_params=pltpu.CompilerParams(vmem_limit_bytes=16 * 1024 * 1024),
        )(recv4, dg, full, zh, zl)
        grad_field = df.reshape(batch, rows, lon, chan).transpose(0, 3, 1, 2)
        grad_wmix = dw.reshape(d.lat, chan, 2, chan).transpose(0, 1, 3, 2)
        return grad_field, grad_wmix

    return jax.shard_map(local_step, mesh=mesh, in_specs=(field_spec, field_spec, P(), P(), P()), out_specs=(field_spec, P('member', None, None, None)), check_vma=False)
```

time: 307 us -> 176 us (0.57)
  waiting for transfers between devices: 53.5 us -> 0 us
  local copies, waits for them, and re-layouts: 36.7 us -> 0.02 us
  Pallas kernels: 202 us -> 175 us
  between operations: 14.1 us -> 0.69 us
    all_gather x1 -> x0, waiting for transfers between devices: 53.5 us -> none  [local_step(): lax.all_gather(dw.reshape(d.t, 1, 2 * chan, chan), 'lat', axis=1, tiled=T...]
    pallas_call x6 -> x2, Pallas kernels: 202 us -> 175 us  [the longest x1 169 us: local_step(): pl.pallas_call(functools.partial(main_kernel, d), name='main', out_shape=...]
    unnamed x1 -> x6, local copies, waits for them, and re-layouts: 18.6 us -> 0.02 us
    all_gather x1 -> x0, local copies, waits for them, and re-layouts: 16.3 us -> none  [local_step(): lax.all_gather(dw.reshape(d.t, 1, 2 * chan, chan), 'lat', axis=1, tiled=T...]
  transfers between devices with their start and end apart: 1 -> 0, of which waited for: 1 -> 0; matrix products, arithmetic and copies ran while one was open for 0% -> 0% of each run, Pallas kernels for 2% -> 0%
where the time goes in v2:
time: 176 us
  Pallas kernels  175 us (99%)
    pallas_call x1, Pallas kernels, local_step(): pl.pallas_call(functools.partial(main_kernel, d), name='main', out_shape=...  169 us
    pallas_call x1, Pallas kernels, local_step(): pl.pallas_call(functools.partial(final_kernel, d), name='final', out_shap...  6.2 us

profile of v2, /device:TPU:97, one launch (start us, length us, event | category | flops | bytes accessed | tf_op | source)
XLA Modules:
  0.0 175.7 jit_solution(9618515323390161526)
XLA Ops:
  0.6 0.0 copy-start
  0.6 0.0 copy-start.1
  0.7 0.0 copy-start.2
  0.7 168.8 %main.1 = (bf16[32,144,128]{2,1,0:T(8,128)(2,1)S(1)}, f32[3,32,256,128]{3,2,1,0:T(8,128)S(1)}) custom-call(f32[24,192,128]{2,1,0:T(8,128)} %bitcast.18, f32[24,192,128]{2,1,0:T(8,128)} %bitcast.15, f32[24576,128]{1,0:T(8,128)} %bitcast.17, f32[96,96,96]{2,1,0:T(8,128)} %pf_h.1, f32[96,96,96]{2,1,0:T(8,128)} %pi_h.1, bf16[96,96]{1,0:T(8,128)(2,1)} %constant.18.clone.perm, ...), custom_call_target="tpu_custom_call" | custom-call | tf_op jit(solution)/shard_map/main/pallas_call | solution.py:508
  169.4 0.0 copy-done
  169.4 0.0 copy-done.1
  169.5 0.0 copy-done.2
  169.5 6.2 %final.1 = (f32[24,192,128]{2,1,0:T(8,128)}, f32[3,32,256,128]{3,2,1,0:T(8,128)}) custom-call(bf16[32,144,128]{2,1,0:T(8,128)(2,1)S(1)} %get-tuple-element.6.got, f32[24,192,128]{2,1,0:T(8,128)S(1)} %bitcast.16, f32[3,32,256,128]{3,2,1,0:T(8,128)S(1)} %get-tuple-element.7.full, bf16[192,192]{1,0:T(8,128)(2,1)S(1)} %copy-done.2, bf16[192,192]{1,0:T(8,128)(2,1)S(1)} %copy-done.1), custom_call_target="tpu_custom_call" | custom-call | tf_op jit(solution)/shard_map/final/pallas_call | solution.py:520
Async XLA Ops:
  0.6 168.8 %copy-start = (f32[8,128,3,192]{1,3,2,0:T(8,128)S(1)}, f32[8,128,3,192]{1,3,2,0:T(8,128)}, u32[]{:S(2)}) copy-start(f32[8,128,3,192]{1,3,2,0:T(8,128)} %param.15) | copy-start | bytes 7077892
  0.6 168.8 %copy-start.1 = (bf16[192,192]{1,0:T(8,128)(2,1)S(1)}, bf16[192,192]{1,0:T(8,128)(2,1)}, u32[]{:S(2)}) copy-start(bf16[192,192]{1,0:T(8,128)(2,1)} %constant.26.clone.slo) | copy-start | bytes 221188
  0.7 168.8 %copy-start.2 = (bf16[192,192]{1,0:T(8,128)(2,1)S(1)}, bf16[192,192]{1,0:T(8,128)(2,1)}, u32[]{:S(2)}) copy-start(bf16[192,192]{1,0:T(8,128)(2,1)} %constant.25.clone.shi) | copy-start | bytes 221188

commit v3 on v0

v3 whole, which is shorter than its diff:
```python
import functools
import math
import numpy as np
import jax
import jax.numpy as jnp
from jax import lax
from jax.experimental import pallas as pl
from jax.experimental.pallas import tpu as pltpu
from jax.sharding import PartitionSpec as P

MESH = pl.DeviceIdType.MESH
F32, BF16 = jnp.float32, jnp.bfloat16
VMEM = pltpu.VMEM


class Dims:
    def __init__(self, n, batch, chan, rows, lon):
        self.n = n
        self.side = math.isqrt(n // 2)
        self.nc = 2
        self.b, self.c, self.t, self.lon = batch // self.nc, chan, rows, lon
        self.lat = n * rows
        self.bt = self.b * rows
        self.msg = 2 * rows * self.bt
        self.lp = self.lat + 8
        self.ship_off = [self.b * j * (j + 1) for j in range(rows + 1)]


def split_const(mat):
    hi = mat.astype(jnp.bfloat16)
    lo = (mat - hi.astype(np.float64)).astype(jnp.bfloat16)
    return hi, lo


def dft_constants(d):
    m = np.arange(d.lat)
    ang = 2.0 * np.pi * np.outer(m, np.arange(d.lon)) / d.lon
    scale = 1.0 / math.sqrt(d.lon)
    ana = scale * np.concatenate([np.cos(ang), -np.sin(ang)])
    gain = np.where(m == 0, 1.0, 2.0)[:, None]
    ana2 = scale * np.concatenate([np.cos(ang) * gain, -np.sin(ang) * gain])
    syn = ana2.T
    syn2 = ana.T
    return [split_const(a) for a in (ana, ana2, syn, syn2)]


def perm_constant(d):
    t = np.arange(d.lat)
    tau = (t % d.t) * d.n + t // d.t
    mat = np.zeros((d.lat, d.lat))
    mat[t, tau] = 1.0
    return mat.astype(jnp.bfloat16)


def mm(a, b):
    return jnp.dot(a, b, preferred_element_type=F32)


def mm_nt(a, b):
    return lax.dot_general(a, b, (((1,), (1,)), ((), ())), preferred_element_type=F32)


def mm_tn(a, b):
    return lax.dot_general(a, b, (((0,), (0,)), ((), ())), preferred_element_type=F32)


def rnd(x):
    return x.astype(BF16).astype(F32)


class Torus:
    def __init__(self, d, me):
        side = d.side
        y, x, h = me // (2 * side), lax.rem(me // 2, side), lax.rem(me, 2)
        self.side, self.h = side, h
        self.ys = [lax.rem(y + i, side) * (2 * side) for i in range(side)]
        self.xs = [lax.rem(x + i, side) * 2 for i in range(side)]
        self.hs = [h, 1 - h]

    def at(self, dy, dx, dh):
        return self.ys[dy % self.side] + self.xs[dx % self.side] + self.hs[dh % 2]


def remote(src, dst, ssem, rsem, to):
    return pltpu.make_async_remote_copy(src_ref=src, dst_ref=dst, send_sem=ssem, recv_sem=rsem,
                                        device_id={"lat": to}, device_id_type=MESH)


class Exchange:
    def __init__(self, d, me, tor, send, recv, hold, sems):
        self.d, self.me, self.tor, self.send, self.recv, self.hold = d, me, tor, send, recv, hold
        self.ssem, self.rsem, self.hsem, self.fsem = [sems.at[i] for i in range(4)]
        side, half = d.side, d.side // 2
        self.half = half
        chips = [(dy, dx) for dy in range(side) for dx in range(side)]
        self.relayed = [o for o in chips if half in o]
        self.direct = [o + (1,) for o in chips if half not in o] + [o + (0,) for o in chips if o != (0, 0)]

    def hop(self, dy, dx):
        return -int(dy == self.half), -int(dx == self.half)

    def start(self):
        for i, (dy, dx) in enumerate(self.relayed):
            ry, rx = self.hop(dy, dx)
            to, via = self.tor.at(dy, dx, 1), self.tor.at(ry, rx, 0)
            remote(self.send.at[to], self.hold.at[i], self.ssem, self.hsem, via).start()
        for o in self.direct:
            to = self.tor.at(*o)
            remote(self.send.at[to], self.recv.at[self.me], self.ssem, self.rsem, to).start()

    def wait(self, ref, sem):
        pltpu.make_async_copy(ref, ref, sem).wait()

    def forward(self):
        self.wait(self.hold, self.hsem)
        for i, (dy, dx) in enumerate(self.relayed):
            ry, rx = self.hop(dy, dx)
            origin, to = self.tor.at(-ry, -rx, 0), self.tor.at(dy - ry, dx - rx, 1)
            remote(self.hold.at[i], self.recv.at[origin], self.fsem, self.rsem, to).start()

    def collect(self):
        self.recv[self.me] = self.send[self.me]
        self.wait(self.recv.at[0:self.d.n - 1], self.rsem)

    def drain(self):
        self.wait(self.send.at[0:self.d.n - 1], self.ssem)
        self.wait(self.hold, self.fsem)


def message_rows(d, s):
    return pl.ds(pl.multiple_of(s * d.msg, 8), d.msg)


def ring_rows(d, start):
    return pl.ds(start, d.n, stride=d.msg)


def put_modes(d, stage, y, bt, lanes):
    for rk in range(2 * d.t):
        stage[ring_rows(d, rk * d.bt + bt), :] = y[rk * d.n:(rk + 1) * d.n, lanes]


def get_modes(d, stage, bt):
    return jnp.concatenate([stage[ring_rows(d, rk * d.bt + bt), :] for rk in range(2 * d.t)], axis=0)


def analyse(x, hi, lo):
    xh = x.astype(BF16)
    xl = (x - xh.astype(F32)).astype(BF16)
    return mm(hi[...], xh) + mm(lo[...], xh) + mm(hi[...], xl)


def loop(count, body, unroll=1):
    def step(i, _):
        body(i)
        return 0
    lax.fori_loop(0, count, step, 0, unroll=unroll)


def lane_halves(d):
    return slice(0, d.c), slice(d.c, 2 * d.c)


def permuted(d, perm, p, out, outt):
    for k in range(d.t):
        pk = p[k].astype(BF16)
        out[k] = mm(pk, perm[...]).astype(BF16)
        outt[k] = mm_tn(perm[...], pk.T).astype(BF16)


def spec_at(d, r, k, b):
    return pl.multiple_of(((k * 2 + r) * d.b + b) * d.lp + d.n * k, 8)


def to_spectral(d, stage, spec, turn, p, sign):
    for k in range(d.t):
        low = d.n * k

        def body(b):
            x = jnp.concatenate([jnp.concatenate(
                [stage[ring_rows(d, (r * d.t + k) * d.bt + b * d.t + t), :] for t in range(d.t)], axis=0)
                for r in range(2)], axis=1)
            y = rnd(mm(p[k, low:, :], x.astype(BF16)))
            for r, half in enumerate(lane_halves(d)):
                spec[pl.ds(spec_at(d, r, k, b), d.lat - low), :] = y[:, half]
                turn[pl.ds(spec_at(d, 1 - r, k, b), d.lat - low), :] = y[:, half] * (sign if r == 0 else -sign)
        loop(d.b, body, d.b)


def from_spectral(d, spec, stage, pt):
    for k in range(d.t):
        low = d.n * k

        def body(b):
            x = jnp.concatenate([spec[pl.ds(spec_at(d, r, k, b), d.lat - low), :] for r in range(2)], axis=1).astype(BF16)
            y = mm(pt[k][:, low:], x)
            for r, half in enumerate(lane_halves(d)):
                for t in range(d.t):
                    stage[ring_rows(d, (r * d.t + k) * d.bt + b * d.t + t), :] = y[t * d.n:(t + 1) * d.n, half]
        loop(d.b, body, d.b)


def mix(d, spec, turn, out, w, ship, base, forward):
    for j in range(d.t):
        rows = 2 * d.b * (j + 1)

        def body(ll):
            l = d.n * j + ll
            at = pl.ds(l, rows, stride=d.lp)
            x = spec[at, :].astype(BF16)
            ship[ll, base + d.ship_off[j]:base + d.ship_off[j + 1], :] = x
            x2 = jnp.concatenate([x, turn[at, :].astype(BF16)], axis=1)
            if forward:
                y = mm_nt(x2, jnp.concatenate([w[l, :d.c, :], w[l, d.c:, :]], axis=1))
            else:
                y = mm(x2, w[l])
            out[at, :] = rnd(y)
        loop(d.n, body, 8)


def gelu_grad(values):
    cumulative = 0.5 * (1.0 + lax.erf(values * math.sqrt(0.5)))
    density = jnp.exp(-0.5 * values * values) * (1.0 / math.sqrt(2.0 * math.pi))
    return cumulative + values * density


def weights(d, a, dq, out, me):
    size = d.ship_off[-1]
    for j in range(d.t):
        y = 0.0
        for c in range(d.nc):
            at = slice(c * size + d.ship_off[j], c * size + d.ship_off[j + 1])
            groups = d.n * (j + 1)
            x = a[:, at, :].astype(F32).reshape(groups, 2 * d.b, d.c)
            turn = jnp.concatenate([-x[:, d.b:, :], x[:, :d.b, :]], axis=1)
            both = jnp.concatenate([x, turn], axis=2).reshape(groups * 2 * d.b, 2 * d.c)
            g = dq[:, at, :].astype(F32).reshape(groups * 2 * d.b, d.c)
            y = y + mm_tn(g.astype(BF16), both.astype(BF16))
        for r, half in enumerate(lane_halves(d)):
            out[j, me, pl.ds(r, d.c, stride=2), :] = y[:, half]


class Gather:
    def __init__(self, d, me, tor, full, ssem, r1, r2, rp):
        self.d, self.me, self.tor, self.full = d, me, tor, full
        self.ssem, self.r1, self.r2, self.rp = ssem, r1, r2, rp
        self.half = full.shape[2] // 2
        h, side = tor.h, tor.side
        self.first = [lax.select(h == 0, tor.xs[i], tor.ys[i]) for i in range(side)]
        self.second = [lax.select(h == 0, tor.ys[i], tor.xs[i]) for i in range(side)]

    def near(self, one, two):
        return self.first[one % self.d.side] + self.second[two % self.d.side] + self.tor.h

    def piece(self, block, part):
        if part is None:
            return self.full.at[:, block]
        return self.full.at[:, block, self.half * part:self.half * (part + 1), :]

    def start(self, block, part, rsem, to):
        ref = self.piece(block, part)
        remote(ref, ref, self.ssem, rsem, to).start()

    def arrive(self, block, part, rsem):
        ref = self.piece(block, part)
        pltpu.make_async_copy(ref, ref, rsem).wait()

    def run(self, between):
        near, r1, r2, rp = self.near, self.r1, self.r2, self.rp
        partner = self.tor.at(0, 0, 1)
        pos = [0, -1, 1, 2]
        p1, m1, p2, m2 = near(1, 0), near(-1, 0), near(0, 1), near(0, -1)
        group = [near(i, 0) for i in pos]

        def second(q):
            self.start(group[q], None, r2.at[q, 0], p2)
            self.start(group[q], None, r2.at[q, 1], m2)
            self.start(group[q], None, rp.at[q], partner)

        def relay(q):
            for i, (off, to) in enumerate(((-1, p2), (1, m2))):
                block = near(pos[q], off)
                self.arrive(block, None, r2.at[q, i])
                self.start(block, i, r2.at[q, 2 + i], to)
                self.start(block, None, rp.at[4 + 2 * q + i], partner)

        self.start(group[0], None, r1.at[0], p1)
        self.start(group[0], None, r1.at[1], m1)
        second(0)
        between()
        self.arrive(group[1], None, r1.at[0])
        self.start(group[1], 0, r1.at[2], p1)
        second(1)
        self.arrive(group[2], None, r1.at[1])
        self.start(group[2], 1, r1.at[3], m1)
        second(2)
        relay(0)
        self.arrive(group[3], 0, r1.at[2])
        self.arrive(group[3], 1, r1.at[3])
        second(3)
        for q in (1, 2, 3):
            relay(q)
        for q in range(4):
            block = near(pos[q], 2)
            for i in range(2):
                self.arrive(block, i, r2.at[q, 2 + i])
            self.start(block, None, rp.at[12 + q], partner)
        for i in range(16):
            self.arrive(partner, None, rp.at[i])
        every = self.full.at[:, 0:31]
        pltpu.make_async_copy(every, every, self.ssem).wait()


def main_kernel(d, f_h, dg_h, w_h, pf_h, pi_h, perm, ah, al, bh, bl, sh, sl, recv4, full,
                f, dg, w, pf, pi, pw, pwt, pv, pvt, stage, stage2, spec, turn, spec2, send, recv, hold, ship, shipr, shold,
                isem, esem, gsem, r1, r2, rp):
    me = lax.axis_index("lat")
    tor = Torus(d, me)
    bar = pltpu.get_barrier_semaphore()
    loads = [pltpu.make_async_copy(f_h.at[c * d.bt:(c + 1) * d.bt], f.at[c * d.bt:(c + 1) * d.bt], isem.at[c]) for c in range(d.nc)]
    small = []
    for k in range(d.t):
        small.append(pltpu.make_async_copy(pf_h.at[me + k * d.n], pf.at[k], isem.at[d.nc + 2 * k]))
        small.append(pltpu.make_async_copy(pi_h.at[me + k * d.n], pi.at[k], isem.at[d.nc + 2 * k + 1]))
    wloads = [pltpu.make_async_copy(w_h.at[j], full.at[j], isem.at[d.nc + 6 + j]) for j in range(d.t)]
    gload = pltpu.make_async_copy(dg_h, dg, isem.at[d.nc + 6 + d.t])
    for c in loads:
        c.start()

    def greet(k, _):
        pl.semaphore_signal(bar, inc=1, device_id={"lat": lax.rem(me + k, d.n)}, device_id_type=MESH)
        return 0
    lax.fori_loop(1, d.n, greet, 0)

    def exchange(e, snd, rcv, hld):
        return Exchange(d, me, tor, snd, rcv, hld, esem.at[e])

    ex = [[exchange(i * d.nc + c, send.at[i, c], recv.at[i, c] if i < 3 else recv4.at[c], hold.at[i, c])
           for c in range(d.nc)] for i in range(4)]
    ships = [exchange(4 * d.nc + i, ship.at[i], shipr.at[i], shold.at[i]) for i in range(2)]

    def dispatch(i, c, st):
        def fill(s):
            send[i, c, s] = st[message_rows(d, s), :].astype(BF16)
        loop(d.n, fill, 4)
        ex[i][c].start()

    def collect(i, c, st):
        ex[i][c].collect()

        def take(s):
            st[message_rows(d, s), :] = recv[i, c, s].astype(F32)
        loop(d.n, take, 4)

    for c in range(d.nc):
        loads[c].wait()
        if c == 0:
            for x in small + wloads + [gload]:
                x.start()

        def analysis_step(p):
            bt = c * d.bt + 2 * p
            y = analyse(jnp.concatenate([f[bt], f[bt + 1]], axis=1), ah, al)
            for u, half in enumerate(lane_halves(d)):
                put_modes(d, stage, y, 2 * p + u, half)
        loop(d.bt // 2, analysis_step, 3)
        if c == 0:
            pl.semaphore_wait(bar, d.n - 1)
        dispatch(0, c, stage)
    for x in small:
        x.wait()
    permuted(d, perm, pf, pw, pwt)
    permuted(d, perm, pi, pv, pvt)
    ex[0][0].forward()
    for j in range(d.t):
        wloads[j].wait()

        def prepare(ll):
            for r in range(2):
                w[d.n * j + ll, r * d.c:(r + 1) * d.c, :] = full[j, ll, pl.ds(r, d.c, stride=2), :].astype(BF16)
        loop(d.n, prepare, 4)

    for c in range(d.nc):
        collect(0, c, stage2)
        if c + 1 < d.nc:
            ex[0][c + 1].forward()
        to_spectral(d, stage2, spec, turn, pw, 1.0)
        mix(d, spec, turn, spec2, w, ship.at[0], c * d.ship_off[-1], True)
        from_spectral(d, spec2, stage, pvt)
        dispatch(1, c, stage)
    ships[0].start()
    gload.wait()
    ex[1][0].forward()
    for c in range(d.nc):
        collect(1, c, stage2)
        if c + 1 < d.nc:
            ex[1][c + 1].forward()

        def grid_step(p):
            bt = 2 * p
            at = c * d.bt + bt
            g = jnp.concatenate([get_modes(d, stage2, bt), get_modes(d, stage2, bt + 1)], axis=1).astype(BF16)
            h = mm(sh[...], g) + mm(sl[...], g)
            u = jnp.concatenate([dg[at], dg[at + 1]], axis=1) * gelu_grad(h)
            y = analyse(u, bh, bl)
            for i, half in enumerate(lane_halves(d)):
                put_modes(d, stage, y, bt + i, half)
        loop(d.bt // 2, grid_step, 2)
        dispatch(2, c, stage)
    ships[0].forward()
    ex[2][0].forward()
    for c in range(d.nc):
        collect(2, c, stage2)
        if c + 1 < d.nc:
            ex[2][c + 1].forward()
        to_spectral(d, stage2, spec, turn, pv, -1.0)
        mix(d, spec, turn, spec2, w, ship.at[1], c * d.ship_off[-1], False)
        if c + 1 == d.nc:
            ships[1].start()
        from_spectral(d, spec2, stage, pwt)
        dispatch(3, c, stage)
    ships[0].collect()
    ships[1].forward()
    ships[1].collect()
    weights(d, shipr.at[0], shipr.at[1], full, me)
    gather = Gather(d, me, tor, full, gsem.at[0], r1, r2, rp)

    def between():
        for e in ex[3]:
            e.forward()
    gather.run(between)
    for e in ex[3]:
        e.collect()
    for e in sum(ex, []) + ships:
        e.drain()


def final_kernel(d, got, dg_h, full, shi, slo, out, dw, dg, stage, sem):
    copy = pltpu.make_async_copy(full, dw, sem.at[0])
    load = pltpu.make_async_copy(dg_h, dg, sem.at[1])
    load.start()
    copy.start()
    for c in range(d.nc):
        def take(s):
            stage[message_rows(d, s), :] = got[c, s].astype(F32)
        loop(d.n, take, 2)
        if c == 0:
            load.wait()

        def body(p):
            bt = 2 * p
            at = c * d.bt + bt
            g = jnp.concatenate([get_modes(d, stage, bt), get_modes(d, stage, bt + 1)], axis=1).astype(BF16)
            y = mm(shi[...], g) + mm(slo[...], g)
            for i, half in enumerate(lane_halves(d)):
                out[at + i] = dg[at + i] + y[:, half]
        loop(d.bt // 2, body, 2)
    copy.wait()


def solution(mesh):
    n = mesh.shape['lat']
    field_spec = P('member', None, 'lat', None)

    def local_step(field_loc, grad_loc, p_fwd, p_inv, w_mix):
        batch, chan, rows, lon = field_loc.shape
        d = Dims(n, batch, chan, rows, lon)
        (ah, al), (bh, bl), (sh, sl), (zh, zl) = dft_constants(d)
        perm = perm_constant(d)
        f = field_loc.transpose(0, 2, 3, 1).reshape(batch * rows, lon, chan)
        dg = grad_loc.transpose(0, 2, 3, 1).reshape(batch * rows, lon, chan)
        w = w_mix.transpose(0, 1, 3, 2).reshape(rows, n, 2 * chan, chan)

        nr = 2 * d.side - 1
        sl_rows = d.nc * d.ship_off[-1]
        nc, ne = d.nc, 4 * d.nc + 2
        stage = VMEM((n * d.msg, chan), F32)
        spec = VMEM((2 * rows * d.b * d.lp, chan), F32)
        mat = VMEM((rows, d.lat, d.lat), BF16)
        raw = VMEM((rows, d.lat, d.lat), F32)
        field = VMEM(f.shape, F32)
        dma = lambda *s: pltpu.SemaphoreType.DMA(s)
        vspec = pl.BlockSpec(memory_space=VMEM)
        aspec = pl.BlockSpec(memory_space=pl.ANY)
        recv4, full = pl.pallas_call(
            functools.partial(main_kernel, d), name="main",
            out_shape=[VMEM((nc, n, d.msg, chan), BF16), VMEM((rows, n, 2 * chan, chan), F32)],
            in_specs=[aspec] * 5 + [vspec] * 7,
            out_specs=[vspec, vspec],
            scratch_shapes=[field, field, VMEM((d.lat, 2 * chan, chan), BF16), raw, raw, mat, mat, mat, mat, stage, stage, spec, spec, spec,
                            VMEM((4, nc, n, d.msg, chan), BF16), VMEM((3, nc, n, d.msg, chan), BF16), VMEM((4, nc, nr, d.msg, chan), BF16),
                            VMEM((2, n, sl_rows, chan), BF16), VMEM((2, n, sl_rows, chan), BF16), VMEM((2, nr, sl_rows, chan), BF16),
                            dma(nc + 7 + rows), dma(ne, 4), dma(1), dma(4), dma(4, 4), dma(16)],
            compiler_params=pltpu.CompilerParams(collective_id=0, has_side_effects=True, vmem_limit_bytes=38 * 1024 * 1024),
        )(f, dg, w, p_fwd, p_inv, perm, ah, al, bh, bl, sh, sl)
        df, dw = pl.pallas_call(
            functools.partial(final_kernel, d), name="final",
            out_shape=[jax.ShapeDtypeStruct(f.shape, F32), jax.ShapeDtypeStruct(full.shape, F32)],
            in_specs=[vspec, aspec, vspec, vspec, vspec], out_specs=[vspec, aspec],
            scratch_shapes=[field, stage, dma(2)],
            compiler_params=pltpu.CompilerParams(vmem_limit_bytes=16 * 1024 * 1024),
        )(recv4, dg, full, zh, zl)
        grad_field = df.reshape(batch, rows, lon, chan).transpose(0, 3, 1, 2)
        grad_wmix = dw.reshape(d.lat, chan, 2, chan).transpose(0, 1, 3, 2)
        return grad_field, grad_wmix

    return jax.shard_map(local_step, mesh=mesh, in_specs=(field_spec, field_spec, P(), P(), P()), out_specs=(field_spec, P('member', None, None, None)), check_vma=False)
```

time: 493 us -> 159 us (0.32); the launches traced: 483 us -> 158 us
  Pallas kernels: 0 us -> 151 us
  matrix products: 140 us -> 0 us
  waiting for transfers between devices: 116 us -> 0 us
  local copies, waits for them, and re-layouts: 99.9 us -> 6.1 us
  blocking collectives: 51.5 us -> 0 us
  other arithmetic: 44.6 us -> 0 us
  starting transfers between devices: 16.1 us -> 0 us
  between operations: 14.9 us -> 0.68 us
    pallas_call x0 -> x2, Pallas kernels: none -> 151 us  [the longest x1 145 us: local_step(): pl.pallas_call(functools.partial(main_kernel, d), name='main', out_shape=...]
    another operation x23 -> x0, matrix products: 113 us -> none  [the longest x12 59.1 us: synthesis(): return jnp.fft.irfft(jnp.pad(complex_spec, pad_width), n=lon_count, axis=-1)]
    psum x1 -> x0, waiting for transfers between devices: 98.1 us -> none  [local_step(): gw_total = lax.psum(gw_part, 'lat')]
    all_to_all x2 -> x0, blocking collectives: 51.5 us -> none  [the longest x1 28.7 us: local_step(): grad_four_lat = lax.all_to_all(grad_four_own, 'lat', 2, 4, tiled=True)]
    another operation x18 -> x0, local copies, waits for them, and re-layouts: 46.1 us -> none  [the longest x12 42.9 us: synthesis(): return jnp.fft.irfft(jnp.pad(complex_spec, pad_width), n=lon_count, axis=-1)]
    dot_general x7 -> x0, matrix products: 27.2 us -> none  [the longest x1 10.2 us: local_step(): jnp.einsum('bolsm,bilrm->losir', grad_mixed, coeffs, preferred_element_ty...]
    unnamed x29 -> x20, local copies, waits for them, and re-layouts: 28.7 us -> 6.1 us
    another operation x17 -> x0, other arithmetic: 21 us -> none  [the longest x1 8.92 us: local_step(): jnp.stack([gw_total[:, :, 0, :, 0] + gw_total[:, :, 1, :, 1], gw_total[:,...]
  transfers between devices with their start and end apart: 3 -> 0, of which waited for: 2 -> 0; matrix products, arithmetic and copies ran while one was open for 20% -> 0% of each run, Pallas kernels for 0% -> 0%
where the time goes in v3:
time: 159 us; the launch traced here: 158 us
  Pallas kernels  151 us (95%)
  local copies, waits for them, and re-layouts  6.1 us (4%)
    pallas_call x1, Pallas kernels, local_step(): pl.pallas_call(functools.partial(main_kernel, d), name='main', out_shape=...  145 us
    pallas_call x1, Pallas kernels, local_step(): pl.pallas_call(functools.partial(final_kernel, d), name='final', out_shap...  6.36 us
    unnamed x20, local copies, waits for them, and re-layouts  6.1 us

profile of v3, /device:TPU:97, one launch (start us, length us, event | category | flops | bytes accessed | tf_op | source)
XLA Modules:
  0.0 158.2 jit_solution(10478859428804304278)
XLA Ops:
  0.6 0.0 copy-start.1
  0.6 0.9 copy-done.1
  1.5 0.0 copy-start.4
  1.5 0.9 copy-done.4
  2.4 0.0 copy-start.5
  2.4 0.9 copy-done.5
  3.3 0.0 copy-start.6
  3.3 0.9 copy-done.6
  4.2 0.0 copy-start.7
  4.2 0.9 copy-done.7
  5.1 0.0 copy-start.8
  5.1 0.9 copy-done.8
  6.0 0.0 copy-start.9
  6.0 0.7 copy-done.9
  6.7 0.0 copy-start
  6.7 0.0 copy-start.2
  6.7 0.0 copy-start.3
  6.7 145.1 %main.1 = (bf16[2,32,72,128]{3,2,1,0:T(8,128)(2,1)S(1)}, f32[3,32,256,128]{3,2,1,0:T(8,128)S(1)}) custom-call(f32[24,192,128]{2,1,0:T(8,128)} %bitcast.18, f32[24,192,128]{2,1,0:T(8,128)} %bitcast.15, f32[3,32,256,128]{3,2,1,0:T(8,128)} %bitcast.17, f32[96,96,96]{2,1,0:T(8,128)} %pf_h.1, f32[96,96,96]{2,1,0:T(8,128)} %pi_h.1, bf16[96,96]{1,0:T(8,128)(2,1)S(1)} %copy-done.9, ...), custom_call_target="tpu_custom_call" | custom-call | tf_op jit(solution)/shard_map/main/pallas_call | solution.py:485
  151.8 0.0 copy-done
  151.8 0.0 copy-done.2
  151.8 0.0 copy-done.3
  151.8 6.4 %final.1 = (f32[24,192,128]{2,1,0:T(8,128)}, f32[3,32,256,128]{3,2,1,0:T(8,128)}) custom-call(bf16[2,32,72,128]{3,2,1,0:T(8,128)(2,1)S(1)} %get-tuple-element.6.got, f32[24,192,128]{2,1,0:T(8,128)S(1)} %bitcast.16, f32[3,32,256,128]{3,2,1,0:T(8,128)S(1)} %get-tuple-element.7.full, bf16[192,192]{1,0:T(8,128)(2,1)S(1)} %copy-done.3, bf16[192,192]{1,0:T(8,128)(2,1)S(1)} %copy-done.2), custom_call_target="tpu_custom_call" | custom-call | tf_op jit(solution)/shard_map/final/pallas_call | solution.py:496
Async XLA Ops:
  0.6 0.9 copy-start.1
  1.5 0.9 copy-start.4
  2.4 0.9 copy-start.5
  3.3 0.9 copy-start.6
  4.2 0.9 copy-start.7
  5.1 0.9 copy-start.8
  6.0 0.7 copy-start.9
  6.7 145.1 %copy-start = (f32[8,128,3,192]{1,3,2,0:T(8,128)S(1)}, f32[8,128,3,192]{1,3,2,0:T(8,128)}, u32[]{:S(2)}) copy-start(f32[8,128,3,192]{1,3,2,0:T(8,128)} %param.15) | copy-start | bytes 7077892
  6.7 145.1 %copy-start.2 = (bf16[192,192]{1,0:T(8,128)(2,1)S(1)}, bf16[192,192]{1,0:T(8,128)(2,1)}, u32[]{:S(2)}) copy-start(bf16[192,192]{1,0:T(8,128)(2,1)} %constant.26.clone.slo) | copy-start | bytes 221188
  6.7 145.1 %copy-start.3 = (bf16[192,192]{1,0:T(8,128)(2,1)S(1)}, bf16[192,192]{1,0:T(8,128)(2,1)}, u32[]{:S(2)}) copy-start(bf16[192,192]{1,0:T(8,128)(2,1)} %constant.25.clone.shi) | copy-start | bytes 221188

commit v4 on v3

--- a/solution.py
+++ b/solution.py
@@ -87,36 +87,18 @@
 
 
 class Exchange:
-    def __init__(self, d, me, tor, send, recv, hold, sems):
-        self.d, self.me, self.tor, self.send, self.recv, self.hold = d, me, tor, send, recv, hold
-        self.ssem, self.rsem, self.hsem, self.fsem = [sems.at[i] for i in range(4)]
-        side, half = d.side, d.side // 2
-        self.half = half
-        chips = [(dy, dx) for dy in range(side) for dx in range(side)]
-        self.relayed = [o for o in chips if half in o]
-        self.direct = [o + (1,) for o in chips if half not in o] + [o + (0,) for o in chips if o != (0, 0)]
-
-    def hop(self, dy, dx):
-        return -int(dy == self.half), -int(dx == self.half)
+    def __init__(self, d, me, tor, send, recv, sems):
+        self.d, self.me, self.tor, self.send, self.recv = d, me, tor, send, recv
+        self.ssem, self.rsem = sems.at[0], sems.at[1]
+        self.offsets = [(dy, dx, dh) for dy in range(d.side) for dx in range(d.side) for dh in range(2)][1:]
 
     def start(self):
-        for i, (dy, dx) in enumerate(self.relayed):
-            ry, rx = self.hop(dy, dx)
-            to, via = self.tor.at(dy, dx, 1), self.tor.at(ry, rx, 0)
-            remote(self.send.at[to], self.hold.at[i], self.ssem, self.hsem, via).start()
-        for o in self.direct:
+        for o in self.offsets:
             to = self.tor.at(*o)
             remote(self.send.at[to], self.recv.at[self.me], self.ssem, self.rsem, to).start()
 
     def wait(self, ref, sem):
         pltpu.make_async_copy(ref, ref, sem).wait()
-
-    def forward(self):
-        self.wait(self.hold, self.hsem)
-        for i, (dy, dx) in enumerate(self.relayed):
-            ry, rx = self.hop(dy, dx)
-            origin, to = self.tor.at(-ry, -rx, 0), self.tor.at(dy - ry, dx - rx, 1)
-            remote(self.hold.at[i], self.recv.at[origin], self.fsem, self.rsem, to).start()
 
     def collect(self):
         self.recv[self.me] = self.send[self.me]
@@ -124,7 +106,6 @@
 
     def drain(self):
         self.wait(self.send.at[0:self.d.n - 1], self.ssem)
-        self.wait(self.hold, self.fsem)
 
 
 def message_rows(d, s):
@@ -265,7 +246,7 @@
         ref = self.piece(block, part)
         pltpu.make_async_copy(ref, ref, rsem).wait()
 
-    def run(self, between):
+    def run(self):
         near, r1, r2, rp = self.near, self.r1, self.r2, self.rp
         partner = self.tor.at(0, 0, 1)
         pos = [0, -1, 1, 2]
@@ -287,7 +268,6 @@
         self.start(group[0], None, r1.at[0], p1)
         self.start(group[0], None, r1.at[1], m1)
         second(0)
-        between()
         self.arrive(group[1], None, r1.at[0])
         self.start(group[1], 0, r1.at[2], p1)
         second(1)
@@ -311,20 +291,22 @@
         pltpu.make_async_copy(every, every, self.ssem).wait()
 
 
-def main_kernel(d, f_h, dg_h, w_h, pf_h, pi_h, perm, ah, al, bh, bl, sh, sl, recv4, full,
-                f, dg, w, pf, pi, pw, pwt, pv, pvt, stage, stage2, spec, turn, spec2, send, recv, hold, ship, shipr, shold,
+def main_kernel(d, f_h, dg_h, w_h, pf_h, pi_h, perm_h, dft_h, recv4, full,
+                perm, dft, f, dg, w, pf, pi, pw, pwt, pv, pvt, stage, stage2, spec, turn, spec2, send, recv, ship, shipr,
                 isem, esem, gsem, r1, r2, rp):
     me = lax.axis_index("lat")
     tor = Torus(d, me)
     bar = pltpu.get_barrier_semaphore()
     loads = [pltpu.make_async_copy(f_h.at[c * d.bt:(c + 1) * d.bt], f.at[c * d.bt:(c + 1) * d.bt], isem.at[c]) for c in range(d.nc)]
-    small = []
+    ah, al, bh, bl, sh, sl = [dft.at[i] for i in range(6)]
+    tables = pltpu.make_async_copy(dft_h, dft, isem.at[d.nc + 7 + d.t])
+    small = [pltpu.make_async_copy(perm_h, perm, isem.at[d.nc + 8 + d.t])]
     for k in range(d.t):
         small.append(pltpu.make_async_copy(pf_h.at[me + k * d.n], pf.at[k], isem.at[d.nc + 2 * k]))
         small.append(pltpu.make_async_copy(pi_h.at[me + k * d.n], pi.at[k], isem.at[d.nc + 2 * k + 1]))
     wloads = [pltpu.make_async_copy(w_h.at[j], full.at[j], isem.at[d.nc + 6 + j]) for j in range(d.t)]
     gload = pltpu.make_async_copy(dg_h, dg, isem.at[d.nc + 6 + d.t])
-    for c in loads:
+    for c in loads[:1] + [tables] + loads[1:]:
         c.start()
 
     def greet(k, _):
@@ -332,12 +314,12 @@
         return 0
     lax.fori_loop(1, d.n, greet, 0)
 
-    def exchange(e, snd, rcv, hld):
-        return Exchange(d, me, tor, snd, rcv, hld, esem.at[e])
-
-    ex = [[exchange(i * d.nc + c, send.at[i, c], recv.at[i, c] if i < 3 else recv4.at[c], hold.at[i, c])
+    def exchange(e, snd, rcv):
+        return Exchange(d, me, tor, snd, rcv, esem.at[e])
+
+    ex = [[exchange(i * d.nc + c, send.at[i, c], recv.at[i, c] if i < 3 else recv4.at[c])
            for c in range(d.nc)] for i in range(4)]
-    ships = [exchange(4 * d.nc + i, ship.at[i], shipr.at[i], shold.at[i]) for i in range(2)]
+    ships = [exchange(4 * d.nc + i, ship.at[i], shipr.at[i]) for i in range(2)]
 
     def dispatch(i, c, st):
         def fill(s):
@@ -355,6 +337,7 @@
     for c in range(d.nc):
         loads[c].wait()
         if c == 0:
+            tables.wait()
             for x in small + wloads + [gload]:
                 x.start()
 
@@ -371,7 +354,6 @@
         x.wait()
     permuted(d, perm, pf, pw, pwt)
     permuted(d, perm, pi, pv, pvt)
-    ex[0][0].forward()
     for j in range(d.t):
         wloads[j].wait()
 
@@ -382,19 +364,14 @@
 
     for c in range(d.nc):
         collect(0, c, stage2)
-        if c + 1 < d.nc:
-            ex[0][c + 1].forward()
         to_spectral(d, stage2, spec, turn, pw, 1.0)
         mix(d, spec, turn, spec2, w, ship.at[0], c * d.ship_off[-1], True)
         from_spectral(d, spec2, stage, pvt)
         dispatch(1, c, stage)
     ships[0].start()
     gload.wait()
-    ex[1][0].forward()
     for c in range(d.nc):
         collect(1, c, stage2)
-        if c + 1 < d.nc:
-            ex[1][c + 1].forward()
 
         def grid_step(p):
             bt = 2 * p
@@ -407,12 +384,8 @@
                 put_modes(d, stage, y, bt + i, half)
         loop(d.bt // 2, grid_step, 2)
         dispatch(2, c, stage)
-    ships[0].forward()
-    ex[2][0].forward()
     for c in range(d.nc):
         collect(2, c, stage2)
-        if c + 1 < d.nc:
-            ex[2][c + 1].forward()
         to_spectral(d, stage2, spec, turn, pv, -1.0)
         mix(d, spec, turn, spec2, w, ship.at[1], c * d.ship_off[-1], False)
         if c + 1 == d.nc:
@@ -420,31 +393,31 @@
         from_spectral(d, spec2, stage, pwt)
         dispatch(3, c, stage)
     ships[0].collect()
-    ships[1].forward()
     ships[1].collect()
     weights(d, shipr.at[0], shipr.at[1], full, me)
     gather = Gather(d, me, tor, full, gsem.at[0], r1, r2, rp)
 
-    def between():
-        for e in ex[3]:
-            e.forward()
-    gather.run(between)
+    gather.run()
     for e in ex[3]:
         e.collect()
     for e in sum(ex, []) + ships:
         e.drain()
 
 
-def final_kernel(d, got, dg_h, full, shi, slo, out, dw, dg, stage, sem):
+def final_kernel(d, got, dg_h, full, dft_h, out, dw, dg, stage, dft, sem):
     copy = pltpu.make_async_copy(full, dw, sem.at[0])
     load = pltpu.make_async_copy(dg_h, dg, sem.at[1])
+    tables = pltpu.make_async_copy(dft_h, dft, sem.at[2])
+    tables.start()
     load.start()
     copy.start()
+    shi, slo = dft.at[0], dft.at[1]
     for c in range(d.nc):
         def take(s):
             stage[message_rows(d, s), :] = got[c, s].astype(F32)
         loop(d.n, take, 2)
         if c == 0:
+            tables.wait()
             load.wait()
 
         def body(p):
@@ -465,13 +438,12 @@
     def local_step(field_loc, grad_loc, p_fwd, p_inv, w_mix):
         batch, chan, rows, lon = field_loc.shape
         d = Dims(n, batch, chan, rows, lon)
-        (ah, al), (bh, bl), (sh, sl), (zh, zl) = dft_constants(d)
+        tables = np.stack([m for pair in dft_constants(d) for m in pair])
         perm = perm_constant(d)
         f = field_loc.transpose(0, 2, 3, 1).reshape(batch * rows, lon, chan)
         dg = grad_loc.transpose(0, 2, 3, 1).reshape(batch * rows, lon, chan)
         w = w_mix.transpose(0, 1, 3, 2).reshape(rows, n, 2 * chan, chan)
 
-        nr = 2 * d.side - 1
         sl_rows = d.nc * d.ship_off[-1]
         nc, ne = d.nc, 4 * d.nc + 2
         stage = VMEM((n * d.msg, chan), F32)
@@ -481,25 +453,25 @@
         field = VMEM(f.shape, F32)
         dma = lambda *s: pltpu.SemaphoreType.DMA(s)
         vspec = pl.BlockSpec(memory_space=VMEM)
-        aspec = pl.BlockSpec(memory_space=pl.ANY)
+        hspec = pl.BlockSpec(memory_space=pltpu.HBM)
         recv4, full = pl.pallas_call(
             functools.partial(main_kernel, d), name="main",
             out_shape=[VMEM((nc, n, d.msg, chan), BF16), VMEM((rows, n, 2 * chan, chan), F32)],
-            in_specs=[aspec] * 5 + [vspec] * 7,
+            in_specs=[hspec] * 7,
             out_specs=[vspec, vspec],
-            scratch_shapes=[field, field, VMEM((d.lat, 2 * chan, chan), BF16), raw, raw, mat, mat, mat, mat, stage, stage, spec, spec, spec,
-                            VMEM((4, nc, n, d.msg, chan), BF16), VMEM((3, nc, n, d.msg, chan), BF16), VMEM((4, nc, nr, d.msg, chan), BF16),
-                            VMEM((2, n, sl_rows, chan), BF16), VMEM((2, n, sl_rows, chan), BF16), VMEM((2, nr, sl_rows, chan), BF16),
-                            dma(nc + 7 + rows), dma(ne, 4), dma(1), dma(4), dma(4, 4), dma(16)],
-            compiler_params=pltpu.CompilerParams(collective_id=0, has_side_effects=True, vmem_limit_bytes=38 * 1024 * 1024),
-        )(f, dg, w, p_fwd, p_inv, perm, ah, al, bh, bl, sh, sl)
+            scratch_shapes=[VMEM(perm.shape, BF16), VMEM(tables[:6].shape, BF16), field, field, VMEM((d.lat, 2 * chan, chan), BF16), raw, raw, mat, mat, mat, mat, stage, stage, spec, spec, spec,
+                            VMEM((4, nc, n, d.msg, chan), BF16), VMEM((3, nc, n, d.msg, chan), BF16),
+                            VMEM((2, n, sl_rows, chan), BF16), VMEM((2, n, sl_rows, chan), BF16),
+                            dma(nc + 9 + rows), dma(ne, 2), dma(1), dma(4), dma(4, 4), dma(16)],
+            compiler_params=pltpu.CompilerParams(collective_id=0, has_side_effects=True, vmem_limit_bytes=50 * 1024 * 1024),
+        )(f, dg, w, p_fwd, p_inv, perm, tables[:6])
         df, dw = pl.pallas_call(
             functools.partial(final_kernel, d), name="final",
             out_shape=[jax.ShapeDtypeStruct(f.shape, F32), jax.ShapeDtypeStruct(full.shape, F32)],
-            in_specs=[vspec, aspec, vspec, vspec, vspec], out_specs=[vspec, aspec],
-            scratch_shapes=[field, stage, dma(2)],
-            compiler_params=pltpu.CompilerParams(vmem_limit_bytes=16 * 1024 * 1024),
-        )(recv4, dg, full, zh, zl)
+            in_specs=[vspec, hspec, vspec, hspec], out_specs=[vspec, hspec],
+            scratch_shapes=[field, stage, VMEM(tables[6:].shape, BF16), dma(3)],
+            compiler_params=pltpu.CompilerParams(vmem_limit_bytes=50 * 1024 * 1024),
+        )(recv4, dg, full, tables[6:])
         grad_field = df.reshape(batch, rows, lon, chan).transpose(0, 3, 1, 2)
         grad_wmix = dw.reshape(d.lat, chan, 2, chan).transpose(0, 1, 3, 2)
         return grad_field, grad_wmix

time: 159 us -> 148 us (0.931)
  Pallas kernels: 151 us -> 138 us
  local copies, waits for them, and re-layouts: 6.1 us -> 8.48 us
    pallas_call x1, Pallas kernels: 145 us -> 127 us  [local_step(): pl.pallas_call(functools.partial(main_kernel, d), name='main', out_shape=...]
    pallas_call x1, Pallas kernels: 6.36 us -> 11.2 us  [local_step(): pl.pallas_call(functools.partial(final_kernel, d), name='final', out_shap...]
    unnamed x20 -> x10, local copies, waits for them, and re-layouts: 6.1 us -> 8.48 us
where the time goes in v4:
time: 148 us; the launch traced here: 147 us
  Pallas kernels  138 us (93%)
  local copies, waits for them, and re-layouts  8.48 us (6%)
    pallas_call x1, Pallas kernels, local_step(): pl.pallas_call(functools.partial(main_kernel, d), name='main', out_shape=...  127 us
    pallas_call x1, Pallas kernels, local_step(): pl.pallas_call(functools.partial(final_kernel, d), name='final', out_shap...  11.2 us
    unnamed x10, local copies, waits for them, and re-layouts  8.48 us

profile of v4, /device:TPU:97, one launch (start us, length us, event | category | flops | bytes accessed | tf_op | source)
XLA Modules:
  0.0 147.4 jit_solution(9293637539270979961)
XLA Ops:
  0.6 0.0 copy-start.4
  0.6 127.1 %main.1 = (bf16[2,32,72,128]{3,2,1,0:T(8,128)(2,1)S(1)}, f32[3,32,256,128]{3,2,1,0:T(8,128)S(1)}) custom-call(f32[24,192,128]{2,1,0:T(8,128)} %bitcast.18, f32[24,192,128]{2,1,0:T(8,128)} %bitcast.15, f32[3,32,256,128]{3,2,1,0:T(8,128)} %bitcast.17, f32[96,96,96]{2,1,0:T(8,128)} %pf_h.1, f32[96,96,96]{2,1,0:T(8,128)} %pi_h.1, ...), custom_call_target="tpu_custom_call" | custom-call | tf_op jit(solution)/shard_map/main/pallas_call | solution.py:457
  127.8 0.0 copy-start
  127.8 4.5 %copy-done = f32[3,32,256,128]{3,2,1,0:T(8,128)} copy-done((f32[3,32,256,128]{3,2,1,0:T(8,128)}, f32[3,32,256,128]{3,2,1,0:T(8,128)S(1)}, u32[]{:S(2)}) %copy-start) | copy-done | bytes 12582936
  132.3 0.0 copy-start.2
  132.3 1.0 copy-done.2
  133.3 0.0 copy-done.4
  133.3 0.0 copy-start.1
  133.3 1.7 %copy-done.1 = f32[8,128,3,192]{1,3,2,0:T(8,128)S(1)} copy-done((f32[8,128,3,192]{1,3,2,0:T(8,128)S(1)}, f32[8,128,3,192]{1,3,2,0:T(8,128)}, u32[]{:S(2)}) %copy-start.1) | copy-done | bytes 2359320
  135.0 0.0 copy-start.3
  135.0 1.3 copy-done.3
  136.2 11.2 %final.1 = (f32[24,192,128]{2,1,0:T(8,128)}, f32[3,32,256,128]{3,2,1,0:T(8,128)}) custom-call(bf16[2,32,72,128]{3,2,1,0:T(8,128)(2,1)S(1)} %copy-done.3, f32[24,192,128]{2,1,0:T(8,128)S(1)} %bitcast.16, f32[3,32,256,128]{3,2,1,0:T(8,128)} %copy-done, bf16[2,192,192]{2,1,0:T(8,128)(2,1)S(1)} %copy-done.4), custom_call_target="tpu_custom_call" | custom-call | tf_op jit(solution)/shard_map/final/pallas_call | solution.py:468
Async XLA Ops:
  0.6 132.7 %copy-start.4 = (bf16[2,192,192]{2,1,0:T(8,128)(2,1)S(1)}, bf16[2,192,192]{2,1,0:T(8,128)(2,1)}, u32[]{:S(2)}) copy-start(bf16[2,192,192]{2,1,0:T(8,128)(2,1)} %constant.8.clone.dft_h) | copy-start | bytes 442372
  127.8 4.5 %copy-start = (f32[3,32,256,128]{3,2,1,0:T(8,128)}, f32[3,32,256,128]{3,2,1,0:T(8,128)S(1)}, u32[]{:S(2)}) copy-start(f32[3,32,256,128]{3,2,1,0:T(8,128)S(1)} %get-tuple-element.7.full) | copy-start | bytes 37748740
  132.3 1.0 copy-start.2
  133.3 1.7 %copy-start.1 = (f32[8,128,3,192]{1,3,2,0:T(8,128)S(1)}, f32[8,128,3,192]{1,3,2,0:T(8,128)}, u32[]{:S(2)}) copy-start(f32[8,128,3,192]{1,3,2,0:T(8,128)} %param.9) | copy-start | bytes 7077892
  135.0 1.3 copy-start.3

commit v5 on v4

--- a/solution.py
+++ b/solution.py
@@ -181,7 +181,14 @@
         loop(d.b, body, d.b)
 
 
-def mix(d, spec, turn, out, w, ship, base, forward):
+def extract(d, spec, ship):
+    for j in range(d.t):
+        def body(ll):
+            ship[ll, d.ship_off[j]:d.ship_off[j + 1], :] = spec[pl.ds(d.n * j + ll, 2 * d.b * (j + 1), stride=d.lp), :].astype(BF16)
+        loop(d.n, body, 8)
+
+
+def mix(d, spec, turn, out, w, forward):
     for j in range(d.t):
         rows = 2 * d.b * (j + 1)
 
@@ -189,7 +196,6 @@
             l = d.n * j + ll
             at = pl.ds(l, rows, stride=d.lp)
             x = spec[at, :].astype(BF16)
-            ship[ll, base + d.ship_off[j]:base + d.ship_off[j + 1], :] = x
             x2 = jnp.concatenate([x, turn[at, :].astype(BF16)], axis=1)
             if forward:
                 y = mm_nt(x2, jnp.concatenate([w[l, :d.c, :], w[l, d.c:, :]], axis=1))
@@ -205,20 +211,17 @@
     return cumulative + values * density
 
 
-def weights(d, a, dq, out, me):
-    size = d.ship_off[-1]
+def weights(d, a, dq):
+    parts = []
     for j in range(d.t):
-        y = 0.0
-        for c in range(d.nc):
-            at = slice(c * size + d.ship_off[j], c * size + d.ship_off[j + 1])
-            groups = d.n * (j + 1)
-            x = a[:, at, :].astype(F32).reshape(groups, 2 * d.b, d.c)
-            turn = jnp.concatenate([-x[:, d.b:, :], x[:, :d.b, :]], axis=1)
-            both = jnp.concatenate([x, turn], axis=2).reshape(groups * 2 * d.b, 2 * d.c)
-            g = dq[:, at, :].astype(F32).reshape(groups * 2 * d.b, d.c)
-            y = y + mm_tn(g.astype(BF16), both.astype(BF16))
-        for r, half in enumerate(lane_halves(d)):
-            out[j, me, pl.ds(r, d.c, stride=2), :] = y[:, half]
+        at = slice(d.ship_off[j], d.ship_off[j + 1])
+        groups = d.n * (j + 1)
+        x = a[:, at, :].astype(F32).reshape(groups, 2 * d.b, d.c)
+        turn = jnp.concatenate([-x[:, d.b:, :], x[:, :d.b, :]], axis=1)
+        both = jnp.concatenate([x, turn], axis=2).reshape(groups * 2 * d.b, 2 * d.c)
+        g = dq[:, at, :].astype(F32).reshape(groups * 2 * d.b, d.c)
+        parts.append(mm_tn(g.astype(BF16), both.astype(BF16)))
+    return parts
 
 
 class Gather:
@@ -246,7 +249,7 @@
         ref = self.piece(block, part)
         pltpu.make_async_copy(ref, ref, rsem).wait()
 
-    def run(self):
+    def run(self, tasks):
         near, r1, r2, rp = self.near, self.r1, self.r2, self.rp
         partner = self.tor.at(0, 0, 1)
         pos = [0, -1, 1, 2]
@@ -268,12 +271,14 @@
         self.start(group[0], None, r1.at[0], p1)
         self.start(group[0], None, r1.at[1], m1)
         second(0)
+        tasks[0]()
         self.arrive(group[1], None, r1.at[0])
         self.start(group[1], 0, r1.at[2], p1)
         second(1)
         self.arrive(group[2], None, r1.at[1])
         self.start(group[2], 1, r1.at[3], m1)
         second(2)
+        tasks[1]()
         relay(0)
         self.arrive(group[3], 0, r1.at[2])
         self.arrive(group[3], 1, r1.at[3])
@@ -291,14 +296,14 @@
         pltpu.make_async_copy(every, every, self.ssem).wait()
 
 
-def main_kernel(d, f_h, dg_h, w_h, pf_h, pi_h, perm_h, dft_h, recv4, full,
-                perm, dft, f, dg, w, pf, pi, pw, pwt, pv, pvt, stage, stage2, spec, turn, spec2, send, recv, ship, shipr,
+def main_kernel(d, f_h, dg_h, w_h, pf_h, pi_h, perm_h, dft_h, df, full,
+                perm, dft, wsum, f, dg, w, pf, pi, pw, pwt, pv, pvt, stage, stage2, spec, turn, spec2, send, recv, ship, shipr,
                 isem, esem, gsem, r1, r2, rp):
     me = lax.axis_index("lat")
     tor = Torus(d, me)
     bar = pltpu.get_barrier_semaphore()
     loads = [pltpu.make_async_copy(f_h.at[c * d.bt:(c + 1) * d.bt], f.at[c * d.bt:(c + 1) * d.bt], isem.at[c]) for c in range(d.nc)]
-    ah, al, bh, bl, sh, sl = [dft.at[i] for i in range(6)]
+    ah, al, bh, bl, sh, sl, zh, zl = [dft.at[i] for i in range(8)]
     tables = pltpu.make_async_copy(dft_h, dft, isem.at[d.nc + 7 + d.t])
     small = [pltpu.make_async_copy(perm_h, perm, isem.at[d.nc + 8 + d.t])]
     for k in range(d.t):
@@ -317,9 +322,9 @@
     def exchange(e, snd, rcv):
         return Exchange(d, me, tor, snd, rcv, esem.at[e])
 
-    ex = [[exchange(i * d.nc + c, send.at[i, c], recv.at[i, c] if i < 3 else recv4.at[c])
+    ex = [[exchange(i * d.nc + c, send.at[i, c], recv.at[i, c])
            for c in range(d.nc)] for i in range(4)]
-    ships = [exchange(4 * d.nc + i, ship.at[i], shipr.at[i]) for i in range(2)]
+    ships = [[exchange((4 + i) * d.nc + c, ship.at[i, c], shipr.at[i, c]) for c in range(d.nc)] for i in range(2)]
 
     def dispatch(i, c, st):
         def fill(s):
@@ -365,10 +370,12 @@
     for c in range(d.nc):
         collect(0, c, stage2)
         to_spectral(d, stage2, spec, turn, pw, 1.0)
-        mix(d, spec, turn, spec2, w, ship.at[0], c * d.ship_off[-1], True)
+        extract(d, spec, ship.at[0, c])
+        mix(d, spec, turn, spec2, w, True)
         from_spectral(d, spec2, stage, pvt)
         dispatch(1, c, stage)
-    ships[0].start()
+    for c in range(d.nc):
+        ships[0][c].start()
     gload.wait()
     for c in range(d.nc):
         collect(1, c, stage2)
@@ -387,48 +394,51 @@
     for c in range(d.nc):
         collect(2, c, stage2)
         to_spectral(d, stage2, spec, turn, pv, -1.0)
-        mix(d, spec, turn, spec2, w, ship.at[1], c * d.ship_off[-1], False)
-        if c + 1 == d.nc:
-            ships[1].start()
+        extract(d, spec, ship.at[1, c])
+        ships[1][c].start()
+        mix(d, spec, turn, spec2, w, False)
         from_spectral(d, spec2, stage, pwt)
         dispatch(3, c, stage)
-    ships[0].collect()
-    ships[1].collect()
-    weights(d, shipr.at[0], shipr.at[1], full, me)
+        if c + 1 == d.nc:
+            for e in ships[0] + ships[1][:c]:
+                e.collect()
+    for c in range(d.nc):
+        if c + 1 == d.nc:
+            ships[1][c].collect()
+        for j, y in enumerate(weights(d, shipr.at[0, c], shipr.at[1, c])):
+            if c + 1 < d.nc:
+                wsum[j] = y if c == 0 else wsum[j] + y
+            else:
+                y = wsum[j] + y
+                for r, half in enumerate(lane_halves(d)):
+                    full[j, me, pl.ds(r, d.c, stride=2), :] = y[:, half]
     gather = Gather(d, me, tor, full, gsem.at[0], r1, r2, rp)
 
-    gather.run()
-    for e in ex[3]:
-        e.collect()
-    for e in sum(ex, []) + ships:
+    def finish(c):
+        def task():
+            collect(3, c, stage2)
+
+            def step(p):
+                bt = 2 * p
+                at = c * d.bt + bt
+                g = jnp.concatenate([get_modes(d, stage2, bt), get_modes(d, stage2, bt + 1)], axis=1).astype(BF16)
+                y = mm(zh[...], g) + mm(zl[...], g)
+                for i, half in enumerate(lane_halves(d)):
+                    df[at + i] = dg[at + i] + y[:, half]
+            loop(d.bt // 2, step, 2)
+        return task
+    gather.run([finish(c) for c in range(d.nc)])
+    for e in sum(ex + ships, []):
         e.drain()
 
 
-def final_kernel(d, got, dg_h, full, dft_h, out, dw, dg, stage, dft, sem):
-    copy = pltpu.make_async_copy(full, dw, sem.at[0])
-    load = pltpu.make_async_copy(dg_h, dg, sem.at[1])
-    tables = pltpu.make_async_copy(dft_h, dft, sem.at[2])
-    tables.start()
-    load.start()
-    copy.start()
-    shi, slo = dft.at[0], dft.at[1]
-    for c in range(d.nc):
-        def take(s):
-            stage[message_rows(d, s), :] = got[c, s].astype(F32)
-        loop(d.n, take, 2)
-        if c == 0:
-            tables.wait()
-            load.wait()
-
-        def body(p):
-            bt = 2 * p
-            at = c * d.bt + bt
-            g = jnp.concatenate([get_modes(d, stage, bt), get_modes(d, stage, bt + 1)], axis=1).astype(BF16)
-            y = mm(shi[...], g) + mm(slo[...], g)
-            for i, half in enumerate(lane_halves(d)):
-                out[at + i] = dg[at + i] + y[:, half]
-        loop(d.bt // 2, body, 2)
-    copy.wait()
+def final_kernel(df, full, out, dw, sem):
+    copies = [pltpu.make_async_copy(full.at[j], dw.at[j], sem.at[j]) for j in range(full.shape[0])]
+    copies.append(pltpu.make_async_copy(df, out, sem.at[full.shape[0]]))
+    for c in copies:
+        c.start()
+    for c in copies:
+        c.wait()
 
 
 def solution(mesh):
@@ -444,8 +454,9 @@
         dg = grad_loc.transpose(0, 2, 3, 1).reshape(batch * rows, lon, chan)
         w = w_mix.transpose(0, 1, 3, 2).reshape(rows, n, 2 * chan, chan)
 
-        sl_rows = d.nc * d.ship_off[-1]
-        nc, ne = d.nc, 4 * d.nc + 2
+        nc = d.nc
+        shipped = VMEM((2, nc, n, d.ship_off[-1], chan), BF16)
+        message = VMEM((4, nc, n, d.msg, chan), BF16)
         stage = VMEM((n * d.msg, chan), F32)
         spec = VMEM((2 * rows * d.b * d.lp, chan), F32)
         mat = VMEM((rows, d.lat, d.lat), BF16)
@@ -454,24 +465,24 @@
         dma = lambda *s: pltpu.SemaphoreType.DMA(s)
         vspec = pl.BlockSpec(memory_space=VMEM)
         hspec = pl.BlockSpec(memory_space=pltpu.HBM)
-        recv4, full = pl.pallas_call(
+        df, full = pl.pallas_call(
             functools.partial(main_kernel, d), name="main",
-            out_shape=[VMEM((nc, n, d.msg, chan), BF16), VMEM((rows, n, 2 * chan, chan), F32)],
+            out_shape=[VMEM(f.shape, F32), VMEM(w.shape, F32)],
             in_specs=[hspec] * 7,
             out_specs=[vspec, vspec],
-            scratch_shapes=[VMEM(perm.shape, BF16), VMEM(tables[:6].shape, BF16), field, field, VMEM((d.lat, 2 * chan, chan), BF16), raw, raw, mat, mat, mat, mat, stage, stage, spec, spec, spec,
-                            VMEM((4, nc, n, d.msg, chan), BF16), VMEM((3, nc, n, d.msg, chan), BF16),
-                            VMEM((2, n, sl_rows, chan), BF16), VMEM((2, n, sl_rows, chan), BF16),
-                            dma(nc + 9 + rows), dma(ne, 2), dma(1), dma(4), dma(4, 4), dma(16)],
-            compiler_params=pltpu.CompilerParams(collective_id=0, has_side_effects=True, vmem_limit_bytes=50 * 1024 * 1024),
-        )(f, dg, w, p_fwd, p_inv, perm, tables[:6])
+            scratch_shapes=[VMEM(perm.shape, BF16), VMEM(tables.shape, BF16), VMEM((rows, chan, 2 * chan), F32), field, field,
+                            VMEM((d.lat, 2 * chan, chan), BF16), raw, raw, mat, mat, mat, mat, stage, stage, spec, spec, spec,
+                            message, message, shipped, shipped,
+                            dma(nc + 9 + rows), dma(6 * nc, 2), dma(1), dma(4), dma(4, 4), dma(16)],
+            compiler_params=pltpu.CompilerParams(collective_id=0, has_side_effects=True, vmem_limit_bytes=49 * 1024 * 1024),
+        )(f, dg, w, p_fwd, p_inv, perm, tables)
         df, dw = pl.pallas_call(
-            functools.partial(final_kernel, d), name="final",
-            out_shape=[jax.ShapeDtypeStruct(f.shape, F32), jax.ShapeDtypeStruct(full.shape, F32)],
-            in_specs=[vspec, hspec, vspec, hspec], out_specs=[vspec, hspec],
-            scratch_shapes=[field, stage, VMEM(tables[6:].shape, BF16), dma(3)],
-            compiler_params=pltpu.CompilerParams(vmem_limit_bytes=50 * 1024 * 1024),
-        )(recv4, dg, full, tables[6:])
+            final_kernel, name="final",
+            out_shape=[jax.ShapeDtypeStruct(f.shape, F32), jax.ShapeDtypeStruct(w.shape, F32)],
+            in_specs=[vspec, vspec], out_specs=[hspec, hspec],
+            scratch_shapes=[dma(rows + 1)],
+            compiler_params=pltpu.CompilerParams(vmem_limit_bytes=1024 * 1024),
+        )(df, full)
         grad_field = df.reshape(batch, rows, lon, chan).transpose(0, 3, 1, 2)
         grad_wmix = dw.reshape(d.lat, chan, 2, chan).transpose(0, 1, 3, 2)
         return grad_field, grad_wmix

time: 148 us -> 133 us (0.90)
  local copies, waits for them, and re-layouts: 8.48 us -> 0 us
  Pallas kernels: 138 us -> 132 us
    unnamed x10 -> x0, local copies, waits for them, and re-layouts: 8.48 us -> none
    pallas_call x1, Pallas kernels: 11.2 us -> 5.35 us  [local_step(): pl.pallas_call(final_kernel, name='final', out_shape=[jax.ShapeDtypeStruc...]
where the time goes in v5:
time: 133 us
  Pallas kernels  132 us (99%)
    pallas_call x1, Pallas kernels, local_step(): pl.pallas_call(functools.partial(main_kernel, d), name='main', out_shape=...  127 us
    pallas_call x1, Pallas kernels, local_step(): pl.pallas_call(final_kernel, name='final', out_shape=[jax.ShapeDtypeStruc...  5.35 us

profile of v5, /device:TPU:97, one launch (start us, length us, event | category | flops | bytes accessed | tf_op | source)
XLA Modules:
  0.0 133.1 jit_solution(6608417308880034810)
XLA Ops:
  0.6 127.1 %main.1 = (f32[24,192,128]{2,1,0:T(8,128)S(1)}, f32[3,32,256,128]{3,2,1,0:T(8,128)S(1)}) custom-call(f32[24,192,128]{2,1,0:T(8,128)} %bitcast.16, f32[24,192,128]{2,1,0:T(8,128)} %bitcast.17, f32[3,32,256,128]{3,2,1,0:T(8,128)} %bitcast.15, f32[96,96,96]{2,1,0:T(8,128)} %pf_h.1, f32[96,96,96]{2,1,0:T(8,128)} %pi_h.1, bf16[96,96]{1,0:T(8,128)(2,1)} %constant.4.clone.perm_h, ...), custom_call_target="tpu_custom_call" | custom-call | tf_op jit(solution)/shard_map/main/pallas_call | solution.py:468
  127.8 5.3 %final.1 = (f32[24,192,128]{2,1,0:T(8,128)}, f32[3,32,256,128]{3,2,1,0:T(8,128)}) custom-call(f32[24,192,128]{2,1,0:T(8,128)S(1)} %get-tuple-element.6.df, f32[3,32,256,128]{3,2,1,0:T(8,128)S(1)} %get-tuple-element.7.full), custom_call_target="tpu_custom_call" | custom-call | tf_op jit(solution)/shard_map/final/pallas_call | solution.py:479

commit v6 on v5

--- a/solution.py
+++ b/solution.py
@@ -1,5 +1,6 @@
 import functools
 import math
+import random
 import numpy as np
 import jax
 import jax.numpy as jnp
@@ -17,6 +18,7 @@
     def __init__(self, n, batch, chan, rows, lon):
         self.n = n
         self.side = math.isqrt(n // 2)
+        self.seed = 0
         self.nc = 2
         self.b, self.c, self.t, self.lon = batch // self.nc, chan, rows, lon
         self.lat = n * rows
@@ -73,8 +75,9 @@
         side = d.side
         y, x, h = me // (2 * side), lax.rem(me // 2, side), lax.rem(me, 2)
         self.side, self.h = side, h
-        self.ys = [lax.rem(y + i, side) * (2 * side) for i in range(side)]
-        self.xs = [lax.rem(x + i, side) * 2 for i in range(side)]
+        way = 1 - 2 * h
+        self.ys = [lax.rem(y + way * i + side, side) * (2 * side) for i in range(side)]
+        self.xs = [lax.rem(x + way * i + side, side) * 2 for i in range(side)]
         self.hs = [h, 1 - h]
 
     def at(self, dy, dx, dh):
@@ -91,6 +94,7 @@
         self.d, self.me, self.tor, self.send, self.recv = d, me, tor, send, recv
         self.ssem, self.rsem = sems.at[0], sems.at[1]
         self.offsets = [(dy, dx, dh) for dy in range(d.side) for dx in range(d.side) for dh in range(2)][1:]
+        random.Random(d.seed).shuffle(self.offsets)
 
     def start(self):
         for o in self.offsets:

time: 133 us -> 126 us (0.947)
  Pallas kernels: 132 us -> 125 us
    pallas_call x1, Pallas kernels: 127 us -> 120 us  [local_step(): pl.pallas_call(functools.partial(main_kernel, d), name='main', out_shape=...]
where the time goes in v6:
time: 126 us
  Pallas kernels  125 us (99%)
    pallas_call x1, Pallas kernels, local_step(): pl.pallas_call(functools.partial(main_kernel, d), name='main', out_shape=...  120 us
    pallas_call x1, Pallas kernels, local_step(): pl.pallas_call(final_kernel, name='final', out_shape=[jax.ShapeDtypeStruc...  5.35 us

profile of v6, /device:TPU:97, one launch (start us, length us, event | category | flops | bytes accessed | tf_op | source)
XLA Modules:
  0.0 125.9 jit_solution(15539861003763223226)
XLA Ops:
  0.6 119.9 %main.1 = (f32[24,192,128]{2,1,0:T(8,128)S(1)}, f32[3,32,256,128]{3,2,1,0:T(8,128)S(1)}) custom-call(f32[24,192,128]{2,1,0:T(8,128)} %bitcast.16, f32[24,192,128]{2,1,0:T(8,128)} %bitcast.17, f32[3,32,256,128]{3,2,1,0:T(8,128)} %bitcast.15, f32[96,96,96]{2,1,0:T(8,128)} %pf_h.1, f32[96,96,96]{2,1,0:T(8,128)} %pi_h.1, bf16[96,96]{1,0:T(8,128)(2,1)} %constant.4.clone.perm_h, ...), custom_call_target="tpu_custom_call" | custom-call | tf_op jit(solution)/shard_map/main/pallas_call | solution.py:472
  120.6 5.3 %final.1 = (f32[24,192,128]{2,1,0:T(8,128)}, f32[3,32,256,128]{3,2,1,0:T(8,128)}) custom-call(f32[24,192,128]{2,1,0:T(8,128)S(1)} %get-tuple-element.6.df, f32[3,32,256,128]{3,2,1,0:T(8,128)S(1)} %get-tuple-element.7.full), custom_call_target="tpu_custom_call" | custom-call | tf_op jit(solution)/shard_map/final/pallas_call | solution.py:483

commit v7 on v6

--- a/solution.py
+++ b/solution.py
@@ -18,7 +18,7 @@
     def __init__(self, n, batch, chan, rows, lon):
         self.n = n
         self.side = math.isqrt(n // 2)
-        self.seed = 0
+        self.seed = 4
         self.nc = 2
         self.b, self.c, self.t, self.lon = batch // self.nc, chan, rows, lon
         self.lat = n * rows
@@ -330,10 +330,13 @@
            for c in range(d.nc)] for i in range(4)]
     ships = [[exchange((4 + i) * d.nc + c, ship.at[i, c], shipr.at[i, c]) for c in range(d.nc)] for i in range(2)]
 
-    def dispatch(i, c, st):
+    def pack(i, c, st):
         def fill(s):
             send[i, c, s] = st[message_rows(d, s), :].astype(BF16)
         loop(d.n, fill, 4)
+
+    def dispatch(i, c, st):
+        pack(i, c, st)
         ex[i][c].start()
 
     def collect(i, c, st):
@@ -356,9 +359,10 @@
             for u, half in enumerate(lane_halves(d)):
                 put_modes(d, stage, y, 2 * p + u, half)
         loop(d.bt // 2, analysis_step, 3)
-        if c == 0:
-            pl.semaphore_wait(bar, d.n - 1)
-        dispatch(0, c, stage)
+        pack(0, c, stage)
+    pl.semaphore_wait(bar, d.n - 1)
+    for e in ex[0]:
+        e.start()
     for x in small:
         x.wait()
     permuted(d, perm, pf, pw, pwt)

time: 126 us -> 124 us (0.984)
  Pallas kernels: 125 us -> 123 us
    pallas_call x1, Pallas kernels: 120 us -> 118 us  [local_step(): pl.pallas_call(functools.partial(main_kernel, d), name='main', out_shape=...]
where the time goes in v7:
time: 124 us
  Pallas kernels  123 us (99%)
    pallas_call x1, Pallas kernels, local_step(): pl.pallas_call(functools.partial(main_kernel, d), name='main', out_shape=...  118 us
    pallas_call x1, Pallas kernels, local_step(): pl.pallas_call(final_kernel, name='final', out_shape=[jax.ShapeDtypeStruc...  5.35 us

profile of v7, /device:TPU:97, one launch (start us, length us, event | category | flops | bytes accessed | tf_op | source)
XLA Modules:
  0.0 124.1 jit_solution(15418935641306281611)
XLA Ops:
  0.6 118.1 %main.1 = (f32[24,192,128]{2,1,0:T(8,128)S(1)}, f32[3,32,256,128]{3,2,1,0:T(8,128)S(1)}) custom-call(f32[24,192,128]{2,1,0:T(8,128)} %bitcast.16, f32[24,192,128]{2,1,0:T(8,128)} %bitcast.17, f32[3,32,256,128]{3,2,1,0:T(8,128)} %bitcast.15, f32[96,96,96]{2,1,0:T(8,128)} %pf_h.1, f32[96,96,96]{2,1,0:T(8,128)} %pi_h.1, bf16[96,96]{1,0:T(8,128)(2,1)} %constant.4.clone.perm_h, ...), custom_call_target="tpu_custom_call" | custom-call | tf_op jit(solution)/shard_map/main/pallas_call | solution.py:476
  118.7 5.3 %final.1 = (f32[24,192,128]{2,1,0:T(8,128)}, f32[3,32,256,128]{3,2,1,0:T(8,128)}) custom-call(f32[24,192,128]{2,1,0:T(8,128)S(1)} %get-tuple-element.6.df, f32[3,32,256,128]{3,2,1,0:T(8,128)S(1)} %get-tuple-element.7.full), custom_call_target="tpu_custom_call" | custom-call | tf_op jit(solution)/shard_map/final/pallas_call | solution.py:487

commit v8 on v7

--- a/solution.py
+++ b/solution.py
@@ -282,11 +282,11 @@
         self.arrive(group[2], None, r1.at[1])
         self.start(group[2], 1, r1.at[3], m1)
         second(2)
-        tasks[1]()
         relay(0)
         self.arrive(group[3], 0, r1.at[2])
         self.arrive(group[3], 1, r1.at[3])
         second(3)
+        tasks[1]()
         for q in (1, 2, 3):
             relay(q)
         for q in range(4):

time: 124 us -> 124 us (level)
  no operation moved by 1% of the time
where the time goes in v8:
time: 124 us
  Pallas kernels  123 us (99%)
    pallas_call x1, Pallas kernels, local_step(): pl.pallas_call(functools.partial(main_kernel, d), name='main', out_shape=...  118 us
    pallas_call x1, Pallas kernels, local_step(): pl.pallas_call(final_kernel, name='final', out_shape=[jax.ShapeDtypeStruc...  5.35 us

profile of v8, /device:TPU:97, one launch (start us, length us, event | category | flops | bytes accessed | tf_op | source)
XLA Modules:
  0.0 124.1 jit_solution(4387336293431909884)
XLA Ops:
  0.6 118.1 %main.1 = (f32[24,192,128]{2,1,0:T(8,128)S(1)}, f32[3,32,256,128]{3,2,1,0:T(8,128)S(1)}) custom-call(f32[24,192,128]{2,1,0:T(8,128)} %bitcast.16, f32[24,192,128]{2,1,0:T(8,128)} %bitcast.17, f32[3,32,256,128]{3,2,1,0:T(8,128)} %bitcast.15, f32[96,96,96]{2,1,0:T(8,128)} %pf_h.1, f32[96,96,96]{2,1,0:T(8,128)} %pi_h.1, bf16[96,96]{1,0:T(8,128)(2,1)} %constant.4.clone.perm_h, ...), custom_call_target="tpu_custom_call" | custom-call | tf_op jit(solution)/shard_map/main/pallas_call | solution.py:476
  118.7 5.3 %final.1 = (f32[24,192,128]{2,1,0:T(8,128)}, f32[3,32,256,128]{3,2,1,0:T(8,128)}) custom-call(f32[24,192,128]{2,1,0:T(8,128)S(1)} %get-tuple-element.6.df, f32[3,32,256,128]{3,2,1,0:T(8,128)S(1)} %get-tuple-element.7.full), custom_call_target="tpu_custom_call" | custom-call | tf_op jit(solution)/shard_map/final/pallas_call | solution.py:487
